TPU v7x, 32 devices: a whole 2x2x4 slice. The times are simulated.
32 devices in a mesh: rays: 2 (over x), freq: 16 (over z, y, core).
Axes of the slice: x: 2, y: 2, z: 4, core: 2. Of those that a mesh axis runs over, the one named last changes fastest.
Arguments:
- spectra: bfloat16 [32, 2, 1024, 1024], P(('rays', 'freq')), parts along dimension 0, may hold values from -6 to 6
- wavelet: float32 [16, 2], P('freq'), may hold values from -6 to 6
- freq_index: int32 [16], P('freq'), may hold values from 0 to 15, each once
- slowness: float32 [16], replicated, may hold values from 0.000222 to 0.000667
- layer_ids: int32 [1], replicated, may hold values from 0 to 15
- ray_slowness: float32 [4], P('rays'), parts along dimension 0, may hold values from -0.0001 to 0.0001
Outputs:
- migrated_image: float32 [2, 1024, 1024], P('rays', 'freq'), parts along dimension 0
There are 2 independent parts, one for each index of `rays`. A program takes and returns all parts, laid end to end along the dimension named above; an argument that names none is the same for every part. Nothing has to cross between parts.
Inputs may be any that keep to these rules, and one draw needn't show every extreme that they name: `freq_index`: each frequency 0 to 15 is held by exactly one slot.
All inputs are finite; a program needn't handle non-finite values.
Results may differ from a plain program's by a relative error of at most 0.0065.
Values sent between devices are 32-bit elements; how exact they have to be, the bound alone decides.
A program may use at most 128 MiB of HBM per device.

v0:
```python
import functools
import math

import jax
import jax.numpy as jnp
from jax import lax
from jax.experimental import pallas as pl
from jax.experimental.pallas import tpu as pltpu
from jax.sharding import PartitionSpec as P

GRID_STEP = 12.5
DEPTH_STEP = 10.0
LOW_FREQUENCY = 5.0
FREQUENCY_BAND = 50.0
DAMPING = 6.0
X_RADIX = 8
LANES = 128
LAG = 2
DEPTH = 4
YTALL = 64
EARLY = 2
MESH = pl.DeviceIdType.MESH

PHASE_SIN = (0.9999998807907104, -0.16666465997695923, 0.008326363749802113, -0.00019062065985053778)
PHASE_COS = (0.9999992251396179, -0.499982088804245, 0.04160428047180176, -0.0013190462486818433)
TURN_SIN = (0.9999992251396179, -0.16665679216384888, 0.008313224650919437, -0.0001852344867074862)
TURN_COS = (
    0.9999999403953552, -0.4999990463256836, 0.041663579642772675, -0.0013853666605427861,
    2.315317397005856e-05,
)


def polynomial(coefs, square):
    value = square * coefs[-1] + coefs[-2]
    for coef in coefs[-3::-1]:
        value = value * square + coef
    return value


def half_sincos(half, sin_coefs, cos_coefs):
    square = half * half
    sine = polynomial(sin_coefs, square) * half
    twice = sine + sine
    return twice * polynomial(cos_coefs, square), 1.0 - twice * sine


def turn_sincos(turns):
    reduced = turns - jnp.floor(turns + 0.5)
    return half_sincos(reduced * math.pi, TURN_SIN, TURN_COS)


def butterfly(parts):
    count = len(parts)
    if count == 1:
        return parts
    even = butterfly(parts[0::2])
    odd = butterfly(parts[1::2])
    low, high = [], []
    for i in range(count // 2):
        er, ei = even[i]
        xr, xi = odd[i]
        if i == 0:
            tr, ti = xr, xi
        elif 4 * i == count:
            tr, ti = -xi, xr
        elif 8 * i == count:
            root = math.sqrt(0.5)
            tr, ti = (xr - xi) * root, (xr + xi) * root
        elif 8 * i == 3 * count:
            root = math.sqrt(0.5)
            tr, ti = (xr + xi) * -root, (xr - xi) * root
        else:
            c = math.cos(2 * math.pi * i / count)
            s = math.sin(2 * math.pi * i / count)
            tr, ti = xr * c - xi * s, xr * s + xi * c
        low.append((er + tr, ei + ti))
        high.append((er - tr, ei - ti))
    return low + high


def kernel(
    groups, radix, pieces, freq_total,
    wavelet, freq_index, slowness, layer_ids, rays, spec_hbm, out_ref,
    spec, zed, ytab, field, xtab, vecs, ybase, image, core_in, pair_in, low_in, high_in, etile, eall,
    load_sem, core_s, core_r, pair_s, pair_r, low_s, low_r, high_s, high_r, e_s, e_r,
):
    rows = spec.shape[1] * spec.shape[2]
    cols = spec.shape[3]
    short = rows // radix
    lines = groups // 4
    me = lax.axis_index("freq")
    core = lax.rem(me, 2)
    pair = lax.rem(me // 2, 2)
    spot = me // 4
    core_peer = me + 1 - 2 * core
    pair_peer = me + 2 - 4 * pair

    barrier = pltpu.get_barrier_semaphore()

    def greet(i, carry):
        pl.semaphore_signal(
            barrier, inc=1, device_id={"freq": lax.rem(me + i, groups)}, device_id_type=MESH
        )
        return carry

    lax.fori_loop(1, groups, greet, 0)

    strips = short // 16
    tiles = cols // LANES

    def load(i):
        window = pl.ds(pl.multiple_of(i * 16, 16), 16)
        return pltpu.make_async_copy(
            spec_hbm.at[:, :, window, :], spec.at[:, :, window, :], load_sem.at[i]
        )

    def start_load(i, carry):
        load(i).start()
        return carry

    lax.fori_loop(0, strips, start_load, 0)

    hertz = freq_index[0, 0].astype(jnp.float32) * (FREQUENCY_BAND / freq_total) + LOW_FREQUENCY
    angular = hertz * (2.0 * math.pi)
    slow = slowness[layer_ids[0, 0]]
    slow_sq = slow * slow
    ray_x = rays[0]
    ray_y = rays[1]
    real_base = (angular * angular - DAMPING * DAMPING) * slow_sq
    imag_arg = 2.0 * angular * DAMPING * slow_sq
    turn_x = hertz * ray_x * GRID_STEP
    turn_y = hertz * ray_y * GRID_STEP
    vertical = jnp.full((YTALL, LANES), slow_sq - ray_x * ray_x - ray_y * ray_y, jnp.float32)
    turn_0 = jnp.sqrt(vertical) * (DEPTH_STEP * hertz)
    wave_re = wavelet[0, 0]
    wave_im = wavelet[0, 1]

    block = cols // X_RADIX
    place = lax.broadcasted_iota(jnp.int32, (X_RADIX, cols), 1)
    outer = lax.broadcasted_iota(jnp.int32, (X_RADIX, cols), 0)
    eighth = lax.rem(place * outer, X_RADIX).astype(jnp.float32) * (1.0 / X_RADIX)
    vec_sin, vec_cos = turn_sincos(eighth + place.astype(jnp.float32) * turn_x)
    vecs[0] = vec_cos
    vecs[1] = vec_sin

    width = cols // pieces
    deep = 32

    def x_table(p):
        at = pl.ds(pl.multiple_of(p * width, LANES), width)
        x = lax.broadcasted_iota(jnp.int32, (deep, width), 1) + p * width
        x = x.astype(jnp.float32) * (1.0 / cols)
        k = lax.broadcasted_iota(jnp.int32, (deep, width), 0)

        def strip_of(strip, carry):
            sine, cosine = turn_sincos((k + strip * deep).astype(jnp.float32) * x)
            for k1 in range(X_RADIX):
                vc = vecs[0, k1 : k1 + 1, at]
                vs = vecs[1, k1 : k1 + 1, at]
                row = pl.ds(pl.multiple_of(strip * deep + k1 * block, deep), deep)
                row_im = pl.ds(pl.multiple_of(strip * deep + k1 * block + cols, deep), deep)
                xtab[row, at] = (cosine * vc - sine * vs).astype(jnp.bfloat16)
                xtab[row_im, at] = (-(cosine * vs) - sine * vc).astype(jnp.bfloat16)
            return carry

        lax.fori_loop(0, block // deep, strip_of, 0, unroll=True)

    x_table(0)

    ytiles = short // LANES

    tall = short // YTALL

    def y_table(step, carry):
        n1 = step // (tall * ytiles)
        strip = lax.rem(step // ytiles, tall)
        tile = lax.rem(step, ytiles)
        n2 = lax.broadcasted_iota(jnp.int32, (YTALL, LANES), 0) + strip * YTALL
        k2 = lax.broadcasted_iota(jnp.int32, (YTALL, LANES), 1) + tile * LANES
        n = n2 * radix + n1
        n = n.astype(jnp.float32)
        turns = k2.astype(jnp.float32) * (n * (1.0 / rows))
        turns = turns - jnp.floor(turns)
        sine, cosine = turn_sincos(turns + n * turn_y + turn_0)
        real = (wave_re * cosine + wave_im * sine).astype(jnp.bfloat16)
        imag_f = wave_re * sine - wave_im * cosine
        imag = imag_f.astype(jnp.bfloat16)
        top = pl.ds(pl.multiple_of(strip * YTALL, YTALL), YTALL)
        bottom = pl.ds(pl.multiple_of(strip * YTALL + short, YTALL), YTALL)
        left = pl.ds(pl.multiple_of(tile * LANES, LANES), LANES)
        right = pl.ds(pl.multiple_of(tile * LANES + short, LANES), LANES)
        ytab[n1, top, left] = real
        ytab[n1, top, right] = (-imag_f).astype(jnp.bfloat16)
        ytab[n1, bottom, left] = imag
        ytab[n1, bottom, right] = real
        return carry

    lax.fori_loop(0, radix * tall * ytiles, y_table, 0, unroll=2)

    step_y = 2.0 * math.pi / (rows * GRID_STEP)
    step_x = 2.0 * math.pi / (cols * GRID_STEP)
    imag_sq = imag_arg * imag_arg
    imag_half = imag_arg * 0.5

    sub = lax.broadcasted_iota(jnp.int32, (short, LANES), 0)
    for k1 in range(radix):
        offset = k1 * short - (rows if k1 >= radix // 2 else 0)
        ky = (sub + offset).astype(jnp.float32) * step_y
        ybase[k1] = real_base - ky * ky

    def shift(strip, total):
        load(strip).wait()
        rows_at = pl.ds(pl.multiple_of(strip * 16, 16), 16)

        def inner(tile, acc):
            at = pl.ds(pl.multiple_of(tile * LANES, LANES), LANES)
            kx = lax.broadcasted_iota(jnp.int32, (16, LANES), 1) + tile * LANES
            kx = jnp.where(kx >= cols // 2, kx - cols, kx).astype(jnp.float32) * step_x
            kx_sq = kx * kx
            parts = []
            for k1 in range(radix):
                a = ybase[k1, rows_at, :] - kx_sq
                m = a * a + imag_sq
                q = 0.5 * (m * lax.rsqrt(m) + jnp.abs(a))
                iq = lax.rsqrt(q)
                g = q * iq
                h = imag_half * iq
                forward = a >= 0.0
                vert_re = jnp.where(forward, g, h)
                vert_im = jnp.where(forward, h, g)
                damp = jnp.exp(vert_im * -DEPTH_STEP)
                sine, cosine = half_sincos(
                    vert_re * (0.5 * DEPTH_STEP), PHASE_SIN, PHASE_COS
                )
                cosine = cosine * damp
                sine = sine * damp
                re = spec[0, k1, rows_at, at].astype(jnp.float32)
                im = spec[1, k1, rows_at, at].astype(jnp.float32)
                new_re = re * cosine - im * sine
                new_im = re * sine + im * cosine
                acc = acc + (new_re * new_re + new_im * new_im)
                parts.append((new_re, new_im))
            for n1, (re, im) in enumerate(butterfly(parts)):
                zed[n1, rows_at, at] = re.astype(jnp.bfloat16)
                low = pl.ds(pl.multiple_of(strip * 16 + short, 16), 16)
                zed[n1, low, at] = im.astype(jnp.bfloat16)
            return acc

        return lax.fori_loop(0, tiles, inner, total, unroll=2)

    energy = lax.fori_loop(0, strips, shift, jnp.zeros((16, LANES), jnp.float32))
    etile[...] = energy[:8] + energy[8:]

    chips = groups // 2

    def y_stage(n1, carry):
        for part in range(cols // 256):
            at = slice(part * 256, part * 256 + 256)
            at_im = slice(cols + part * 256, cols + part * 256 + 256)
            res = jnp.dot(ytab[n1], zed[n1, :, at], preferred_element_type=jnp.float32)
            res = res.astype(jnp.bfloat16)
            field[:, n1, :, at] = res[:short].reshape(chips, 16, 256)
            field[:, n1, :, at_im] = res[short:].reshape(chips, 16, 256)
        return carry

    lax.fori_loop(0, radix, y_stage, 0, unroll=True)

    pl.semaphore_wait(barrier, groups - 1)

    def energy_copy(i):
        return pltpu.make_async_remote_copy(
            src_ref=etile, dst_ref=eall.at[i], send_sem=e_s.at[i], recv_sem=e_r.at[i],
            device_id={"freq": lax.rem(me + i, groups)}, device_id_type=MESH,
        )

    def energy_start(i, carry):
        energy_copy(i).start()
        return carry

    lax.fori_loop(1, groups, energy_start, 0)

    def order(j):
        half = j // 2
        return jnp.where(lax.rem(j, 2) == 0, half, lines - 1 - half)

    def cut_of(p):
        return pl.ds(pl.multiple_of(p * width, LANES), width)

    def core_copy(p, b):
        cut = cut_of(p)
        return pltpu.make_async_remote_copy(
            src_ref=image.at[:, b, 1 - core, :, :, cut], dst_ref=core_in.at[:, b, :, :, cut],
            send_sem=core_s.at[p, b], recv_sem=core_r.at[p, b],
            device_id={"freq": core_peer}, device_id_type=MESH,
        )

    def pair_copy(a, p):
        cut = cut_of(p)
        return pltpu.make_async_remote_copy(
            src_ref=image.at[a, 1 - pair, core, :, :, cut], dst_ref=pair_in.at[a, :, :, cut],
            send_sem=pair_s.at[a, p], recv_sem=pair_r.at[a, p],
            device_id={"freq": pair_peer}, device_id_type=MESH,
        )

    def low_copy(a, p):
        cut = cut_of(p)
        return pltpu.make_async_remote_copy(
            src_ref=image.at[a, pair, core, :, :, cut], dst_ref=low_in.at[a, :, :, cut],
            send_sem=low_s.at[a, p], recv_sem=low_r.at[a, p],
            device_id={"freq": jnp.minimum(spot + 1, lines - 1) * 4 + pair * 2 + core},
            device_id_type=MESH,
        )

    def high_copy(a, p):
        cut = cut_of(p)
        return pltpu.make_async_remote_copy(
            src_ref=image.at[a, pair, core, :, :, cut], dst_ref=high_in.at[a, :, :, cut],
            send_sem=high_s.at[a, p], recv_sem=high_r.at[a, p],
            device_id={"freq": jnp.maximum(spot - 1, 0) * 4 + pair * 2 + core},
            device_id_type=MESH,
        )

    count = lines * pieces
    depth = min(DEPTH, count)

    def split(i):
        return order(lax.rem(i, lines)), i // lines

    def first_of(i):
        return lax.rem(i, lines) == 0

    def send_pair(i):
        a, p = split(i)
        cut = cut_of(p)

        @pl.when(first_of(i))
        def _():
            core_copy(p, 1 - pair).wait_recv()

        image[a, 1 - pair, core, :, :, cut] = (
            image[a, 1 - pair, core, :, :, cut] + core_in[a, 1 - pair, :, :, cut]
        )
        pair_copy(a, p).start()

    def third(i, carry):
        @pl.when(i < count)
        def _():
            a, p = split(jnp.minimum(i, count - 1))
            cut = cut_of(p)
            pair_copy(a, p).wait_recv()

            @pl.when(i + depth < count)
            def _():
                send_pair(jnp.minimum(i + depth, count - 1))

            @pl.when(first_of(i))
            def _():
                core_copy(p, pair).wait_recv()

            image[a, pair, core, :, :, cut] = (
                image[a, pair, core, :, :, cut] + core_in[a, pair, :, :, cut] + pair_in[a, :, :, cut]
            )

        upward = i - LAG * spot
        a_up, p_up = split(jnp.clip(upward, 0, count - 1))

        @pl.when((upward >= 0) & (upward < count) & (a_up > spot))
        def _():
            cut = cut_of(p_up)

            @pl.when(spot > 0)
            def _():
                low_copy(a_up, p_up).wait_recv()
                image[a_up, pair, core, :, :, cut] = image[a_up, pair, core, :, :, cut] + low_in[a_up, :, :, cut]

            low_copy(a_up, p_up).start()

        downward = i - LAG * (lines - 1 - spot)
        a_dn, p_dn = split(jnp.clip(downward, 0, count - 1))

        @pl.when((downward >= 0) & (downward < count) & (a_dn < spot))
        def _():
            cut = cut_of(p_dn)

            @pl.when(spot < lines - 1)
            def _():
                high_copy(a_dn, p_dn).wait_recv()
                image[a_dn, pair, core, :, :, cut] = image[a_dn, pair, core, :, :, cut] + high_in[a_dn, :, :, cut]

            high_copy(a_dn, p_dn).start()

        return carry

    def compute(p, carry):
        at = cut_of(p)

        @pl.when(p > 0)
        def _():
            x_table(p)

        @pl.when(p == 1)
        def _():
            lax.fori_loop(0, depth, lambda i, c: (send_pair(i), c)[1], 0)

        lax.fori_loop(EARLY * jnp.maximum(p - 2, 0), EARLY * jnp.maximum(p - 1, 0), third, 0)

        half = max(lines // 4, 1)
        for q in range(lines // half):
            lhs = field[2 * half * q : 2 * half * (q + 1)].reshape(half * 2 * radix * 16, 2 * cols)
            res = jnp.dot(lhs, xtab[:, at], preferred_element_type=jnp.float32)
            res = res.reshape(half, 2, radix, 2, 8, width)
            for c in range(2):
                image[half * q : half * (q + 1), :, c, :, :, at] = res[:, :, :, c]
        core_copy(p, 1 - pair).start()
        core_copy(p, pair).start()
        return carry

    lax.fori_loop(0, pieces, compute, 0)

    lax.fori_loop(EARLY * max(pieces - 2, 0), count + LAG * (lines - 1), third, 0)

    def energy_take(i, total):
        energy_copy(i).wait_recv()
        return total + eall[i]

    total = lax.fori_loop(1, groups, energy_take, etile[...])
    total = jnp.sum(jnp.sum(total, axis=0, keepdims=True), axis=1, keepdims=True)
    scale = lax.rsqrt(total / freq_total + 1e-06)

    def own(p, carry):
        cut = cut_of(p)

        @pl.when(spot > 0)
        def _():
            low_copy(spot, p).wait_recv()
            image[spot, pair, core, :, :, cut] = image[spot, pair, core, :, :, cut] + low_in[spot, :, :, cut]

        @pl.when(spot < lines - 1)
        def _():
            high_copy(spot, p).wait_recv()
            image[spot, pair, core, :, :, cut] = image[spot, pair, core, :, :, cut] + high_in[spot, :, :, cut]

        return carry

    lax.fori_loop(0, pieces, own, 0)
    for n1 in range(radix):
        out_ref[:, n1, :] = image[spot, pair, core, n1] * scale

    def energy_end(i, carry):
        energy_copy(i).wait_send()
        return carry

    lax.fori_loop(1, groups, energy_end, 0)

    def finish_core(p, carry):
        core_copy(p, 0).wait_send()
        core_copy(p, 1).wait_send()
        return carry

    lax.fori_loop(0, pieces, finish_core, 0)

    def finish(a, carry):
        def piece(p, inner):
            pair_copy(a, p).wait_send()

            @pl.when(a > spot)
            def _():
                low_copy(a, p).wait_send()

            @pl.when(a < spot)
            def _():
                high_copy(a, p).wait_send()

            return inner

        return lax.fori_loop(0, pieces, piece, carry)

    lax.fori_loop(0, lines, finish, 0)


def body(spectra, wavelet, freq_index, slowness, layer_ids, ray_slowness):
    slot_total, unused, rows, cols = spectra.shape
    groups = lax.axis_size("freq")
    freq_total = slot_total * groups
    radix = rows // groups // 8
    short = rows // radix
    lines = groups // 4
    pieces = min(4, cols // LANES)
    f32, bf16 = jnp.float32, jnp.bfloat16
    dma = pltpu.SemaphoreType.DMA
    out = pl.pallas_call(
        functools.partial(kernel, groups, radix, pieces, freq_total),
        out_shape=jax.ShapeDtypeStruct((8, radix, cols), f32),
        in_specs=[
            *[pl.BlockSpec(memory_space=pltpu.SMEM)] * 5,
            pl.BlockSpec(memory_space=pl.ANY),
        ],
        out_specs=pl.BlockSpec(memory_space=pltpu.VMEM),
        scratch_shapes=[
            pltpu.VMEM((2, radix, short, cols), bf16),
            pltpu.VMEM((radix, 2 * short, cols), bf16),
            pltpu.VMEM((radix, 2 * short, 2 * short), bf16),
            pltpu.VMEM((groups // 2, radix, 16, 2 * cols), bf16),
            pltpu.VMEM((2 * cols, cols), bf16),
            pltpu.VMEM((2, X_RADIX, cols), f32),
            pltpu.VMEM((radix, short, LANES), f32),
            pltpu.VMEM((lines, 2, 2, radix, 8, cols), f32),
            pltpu.VMEM((lines, 2, radix, 8, cols), f32),
            pltpu.VMEM((lines, radix, 8, cols), f32),
            pltpu.VMEM((lines, radix, 8, cols), f32),
            pltpu.VMEM((lines, radix, 8, cols), f32),
            pltpu.VMEM((8, LANES), f32),
            pltpu.VMEM((groups, 8, LANES), f32),
            dma((short // 16,)),
            dma((pieces, 2)),
            dma((pieces, 2)),
            dma((lines, pieces)),
            dma((lines, pieces)),
            dma((lines, pieces)),
            dma((lines, pieces)),
            dma((lines, pieces)),
            dma((lines, pieces)),
            dma((groups,)),
            dma((groups,)),
        ],
        compiler_params=pltpu.CompilerParams(
            collective_id=0, has_side_effects=True, vmem_limit_bytes=60 * 1024 * 1024
        ),
    )(
        wavelet, freq_index.reshape(1, 1), slowness, layer_ids.reshape(1, 1), ray_slowness,
        spectra.reshape(2, radix, short, cols),
    )
    return out.reshape(1, 8 * radix, cols)


def solution(mesh):
    placed = (
        P(("rays", "freq"), None, None, None),
        P("freq", None),
        P("freq"),
        P(),
        P(),
        P("rays"),
    )
    return jax.shard_map(
        body, mesh=mesh, in_specs=placed, out_specs=P("rays", "freq", None), check_vma=False
    )
```

profile of v0, /device:TPU:0, one launch (start us, length us, event | category | flops | bytes accessed | tf_op | source)
XLA Modules:
  0.0 55.3 jit_solution(1960859113248202471)
XLA Ops:
  1.3 52.3 %shard_map.64 = f32[8,8,1024]{2,1,0:T(8,128)} custom-call(f32[1,2]{1,0:T(1,128)} %wavelet.1, s32[1,1]{1,0:T(1,128)} %bitcast.4.freq_index, f32[16]{0:T(128)} %slowness.1, s32[1,1]{1,0:T(1,128)} %bitcast.5.layer_ids, f32[2]{0:T(128)} %rays.1, bf16[2,8,128,1024]{3,2,1,0:T(8,128)(2,1)} %bitcast.6), custom_call_target="tpu_custom_call" | custom-call | tf_op jit(solution)/shard_map/pallas_call | solution.py:491
  53.6 1.7 %copy.10 = f32[1,64,1024]{2,1,0:T(8,128)} copy(f32[1,64,1024]{2,1,0:T(8,128)} %bitcast.7) | data formatting | bytes 524288
where the time goes:
time: 55.4 us; the launch traced here: 55.3 us
  Pallas kernels  52.3 us (94%)
  local copies, waits for them, and re-layouts  1.67 us (3%)
  between operations  1.3 us (2%)
    pallas_call x1, Pallas kernels, body(): pl.pallas_call(functools.partial(kernel, groups, radix, pieces, freq_tota...  52.3 us
    unnamed x1, local copies, waits for them, and re-layouts  1.67 us

commit v1 on v0

--- a/solution.py
+++ b/solution.py
@@ -1,3 +1,4 @@
+import contextlib
 import functools
 import math
 
@@ -21,13 +22,21 @@
 EARLY = 2
 MESH = pl.DeviceIdType.MESH
 
-PHASE_SIN = (0.9999998807907104, -0.16666465997695923, 0.008326363749802113, -0.00019062065985053778)
-PHASE_COS = (0.9999992251396179, -0.499982088804245, 0.04160428047180176, -0.0013190462486818433)
+HALF_SIN = (0.9999998807907104, -0.16666465997695923, 0.008326363749802113, -0.00019062065985053778)
+HALF_COS = (0.9999992251396179, -0.499982088804245, 0.04160428047180176, -0.0013190462486818433)
 TURN_SIN = (0.9999992251396179, -0.16665679216384888, 0.008313224650919437, -0.0001852344867074862)
 TURN_COS = (
     0.9999999403953552, -0.4999990463256836, 0.041663579642772675, -0.0013853666605427861,
     2.315317397005856e-05,
 )
+
+ROOT = math.sqrt(2.0)
+PHASE_SIN = tuple(ROOT * c / 2.0 ** (2 * k + 1) for k, c in enumerate(HALF_SIN))
+PHASE_COS = tuple(ROOT * c / 4.0**k for k, c in enumerate(HALF_COS))
+
+
+def scope(name):
+    return contextlib.nullcontext()
 
 
 def polynomial(coefs, square):
@@ -81,7 +90,7 @@
 def kernel(
     groups, radix, pieces, freq_total,
     wavelet, freq_index, slowness, layer_ids, rays, spec_hbm, out_ref,
-    spec, zed, ytab, field, xtab, vecs, ybase, image, core_in, pair_in, low_in, high_in, etile, eall,
+    spec, zed, ytab, field, xtab, vecs, fac, image, core_in, pair_in, low_in, high_in, etile, eall,
     load_sem, core_s, core_r, pair_s, pair_r, low_s, low_r, high_s, high_r, e_s, e_r,
 ):
     rows = spec.shape[1] * spec.shape[2]
@@ -165,7 +174,8 @@
 
         lax.fori_loop(0, block // deep, strip_of, 0, unroll=True)
 
-    x_table(0)
+    with scope("xt0"):
+        x_table(0)
 
     ytiles = short // LANES
 
@@ -195,18 +205,65 @@
         ytab[n1, bottom, right] = real
         return carry
 
-    lax.fori_loop(0, radix * tall * ytiles, y_table, 0, unroll=2)
-
-    step_y = 2.0 * math.pi / (rows * GRID_STEP)
-    step_x = 2.0 * math.pi / (cols * GRID_STEP)
-    imag_sq = imag_arg * imag_arg
-    imag_half = imag_arg * 0.5
-
-    sub = lax.broadcasted_iota(jnp.int32, (short, LANES), 0)
-    for k1 in range(radix):
-        offset = k1 * short - (rows if k1 >= radix // 2 else 0)
-        ky = (sub + offset).astype(jnp.float32) * step_y
-        ybase[k1] = real_base - ky * ky
+    with scope("ytab"):
+        lax.fori_loop(0, radix * tall * ytiles, y_table, 0, unroll=2)
+
+    half_gain = 0.5 * DEPTH_STEP * DEPTH_STEP
+    step_y = 2.0 * math.pi / (rows * GRID_STEP) * math.sqrt(half_gain)
+    step_x = 2.0 * math.pi / (cols * GRID_STEP) * math.sqrt(half_gain)
+    base = real_base * half_gain
+    imag = imag_arg * half_gain
+    imag_sq = imag * imag
+
+    def factor(a):
+        m = a * a + imag_sq
+        q = m * lax.rsqrt(m) + jnp.abs(a)
+        iq = lax.rsqrt(q)
+        g = q * iq
+        h = imag * iq
+        forward = a >= 0.0
+        vert_re = jnp.where(forward, g, h)
+        vert_im = jnp.where(forward, h, g)
+        damp = jnp.exp2(vert_im * -math.log2(math.e))
+        square = vert_re * vert_re
+        v = polynomial(PHASE_SIN, square) * vert_re
+        w = polynomial(PHASE_COS, square)
+        dv = damp * v
+        return damp - dv * v, dv * w
+
+    def signed(index, extent):
+        return jnp.where(index >= extent // 2, index - extent, index).astype(jnp.float32)
+
+    lane = lax.broadcasted_iota(jnp.int32, (16, LANES), 1)
+    sub = lax.broadcasted_iota(jnp.int32, (16, LANES), 0)
+    kx_sq = []
+    for t in range(tiles // 2):
+        kx = (lane + t * LANES).astype(jnp.float32) * step_x
+        kx_sq.append(kx * kx)
+    edge_y = signed(lane * 16 + sub, rows) * step_y
+    edge_x = cols // 2 * step_x
+    edge = factor(base - edge_x * edge_x - edge_y * edge_y)
+    turned = lax.rem(LANES - lane, LANES)
+    first = lane == 0
+
+    def factors(m, carry):
+        rows_at = pl.ds(pl.multiple_of(m * 16, 16), 16)
+        ky = signed(sub + m * 16, rows) * step_y
+        ybase = base - ky * ky
+        here = jnp.full((16, LANES), m, jnp.int32)
+        after = [jnp.take_along_axis(e, here, axis=1) for e in edge]
+        for t in reversed(range(tiles // 2)):
+            now = factor(ybase - kx_sq[t])
+            for c in range(2):
+                fac[c, rows_at, t * LANES : (t + 1) * LANES] = now[c]
+                back = jnp.take_along_axis(now[c], turned, axis=1)
+                far = tiles - 1 - t
+                fac[c, rows_at, far * LANES : (far + 1) * LANES] = jnp.where(first, after[c], back)
+            after = now
+        return carry
+
+    with scope("factors"):
+        lax.fori_loop(0, rows // 16, factors, 0)
 
     def shift(strip, total):
         load(strip).wait()
@@ -214,41 +271,27 @@
 
         def inner(tile, acc):
             at = pl.ds(pl.multiple_of(tile * LANES, LANES), LANES)
-            kx = lax.broadcasted_iota(jnp.int32, (16, LANES), 1) + tile * LANES
-            kx = jnp.where(kx >= cols // 2, kx - cols, kx).astype(jnp.float32) * step_x
-            kx_sq = kx * kx
             parts = []
             for k1 in range(radix):
-                a = ybase[k1, rows_at, :] - kx_sq
-                m = a * a + imag_sq
-                q = 0.5 * (m * lax.rsqrt(m) + jnp.abs(a))
-                iq = lax.rsqrt(q)
-                g = q * iq
-                h = imag_half * iq
-                forward = a >= 0.0
-                vert_re = jnp.where(forward, g, h)
-                vert_im = jnp.where(forward, h, g)
-                damp = jnp.exp(vert_im * -DEPTH_STEP)
-                sine, cosine = half_sincos(
-                    vert_re * (0.5 * DEPTH_STEP), PHASE_SIN, PHASE_COS
-                )
-                cosine = cosine * damp
-                sine = sine * damp
+                row = pl.ds(pl.multiple_of(strip * 16 + k1 * short, 16), 16)
+                cosine = fac[0, row, at]
+                sine = fac[1, row, at]
                 re = spec[0, k1, rows_at, at].astype(jnp.float32)
                 im = spec[1, k1, rows_at, at].astype(jnp.float32)
                 new_re = re * cosine - im * sine
                 new_im = re * sine + im * cosine
                 acc = acc + (new_re * new_re + new_im * new_im)
-                parts.append((new_re, new_im))
+                parts.append((new_re.astype(jnp.bfloat16), new_im.astype(jnp.bfloat16)))
             for n1, (re, im) in enumerate(butterfly(parts)):
-                zed[n1, rows_at, at] = re.astype(jnp.bfloat16)
+                zed[n1, rows_at, at] = re
                 low = pl.ds(pl.multiple_of(strip * 16 + short, 16), 16)
-                zed[n1, low, at] = im.astype(jnp.bfloat16)
+                zed[n1, low, at] = im
             return acc
 
         return lax.fori_loop(0, tiles, inner, total, unroll=2)
 
-    energy = lax.fori_loop(0, strips, shift, jnp.zeros((16, LANES), jnp.float32))
+    with scope("shift"):
+        energy = lax.fori_loop(0, strips, shift, jnp.zeros((16, LANES), jnp.float32))
     etile[...] = energy[:8] + energy[8:]
 
     chips = groups // 2
@@ -263,9 +306,11 @@
             field[:, n1, :, at_im] = res[short:].reshape(chips, 16, 256)
         return carry
 
-    lax.fori_loop(0, radix, y_stage, 0, unroll=True)
-
-    pl.semaphore_wait(barrier, groups - 1)
+    with scope("ystage"):
+        lax.fori_loop(0, radix, y_stage, 0, unroll=True)
+
+    with scope("barr"):
+        pl.semaphore_wait(barrier, groups - 1)
 
     def energy_copy(i):
         return pltpu.make_async_remote_copy(
@@ -415,9 +460,11 @@
         core_copy(p, pair).start()
         return carry
 
-    lax.fori_loop(0, pieces, compute, 0)
-
-    lax.fori_loop(EARLY * max(pieces - 2, 0), count + LAG * (lines - 1), third, 0)
+    with scope("compute"):
+        lax.fori_loop(0, pieces, compute, 0)
+
+    with scope("third"):
+        lax.fori_loop(EARLY * max(pieces - 2, 0), count + LAG * (lines - 1), third, 0)
 
     def energy_take(i, total):
         energy_copy(i).wait_recv()
@@ -442,7 +489,8 @@
 
         return carry
 
-    lax.fori_loop(0, pieces, own, 0)
+    with scope("own"):
+        lax.fori_loop(0, pieces, own, 0)
     for n1 in range(radix):
         out_ref[:, n1, :] = image[spot, pair, core, n1] * scale
 
@@ -503,7 +551,7 @@
             pltpu.VMEM((groups // 2, radix, 16, 2 * cols), bf16),
             pltpu.VMEM((2 * cols, cols), bf16),
             pltpu.VMEM((2, X_RADIX, cols), f32),
-            pltpu.VMEM((radix, short, LANES), f32),
+            pltpu.VMEM((2, rows, cols), f32),
             pltpu.VMEM((lines, 2, 2, radix, 8, cols), f32),
             pltpu.VMEM((lines, 2, radix, 8, cols), f32),
             pltpu.VMEM((lines, radix, 8, cols), f32),

time: 55.4 us -> 57.8 us (1.043)
  Pallas kernels: 52.3 us -> 54.7 us
    pallas_call x1, Pallas kernels: 52.3 us -> 54.7 us  [body(): pl.pallas_call(functools.partial(kernel, groups, radix, pieces, freq_tota...]
where the time goes in v1:
time: 57.8 us; the launch traced here: 57.7 us
  Pallas kernels  54.7 us (95%)
  local copies, waits for them, and re-layouts  1.67 us (3%)
  between operations  1.3 us (2%)
    pallas_call x1, Pallas kernels, body(): pl.pallas_call(functools.partial(kernel, groups, radix, pieces, freq_tota...  54.7 us
    unnamed x1, local copies, waits for them, and re-layouts  1.67 us

profile of v1, /device:TPU:0, one launch (start us, length us, event | category | flops | bytes accessed | tf_op | source)
XLA Modules:
  0.0 57.7 jit_solution(9998777336985419146)
XLA Ops:
  1.3 54.7 %shard_map.64 = f32[8,8,1024]{2,1,0:T(8,128)} custom-call(f32[1,2]{1,0:T(1,128)} %wavelet.1, s32[1,1]{1,0:T(1,128)} %bitcast.4.freq_index, f32[16]{0:T(128)} %slowness.1, s32[1,1]{1,0:T(1,128)} %bitcast.5.layer_ids, f32[2]{0:T(128)} %rays.1, bf16[2,8,128,1024]{3,2,1,0:T(8,128)(2,1)} %bitcast.6), custom_call_target="tpu_custom_call" | custom-call | tf_op jit(solution)/shard_map/pallas_call | solution.py:539
  56.0 1.7 %copy.10 = f32[1,64,1024]{2,1,0:T(8,128)} copy(f32[1,64,1024]{2,1,0:T(8,128)} %bitcast.7) | data formatting | bytes 524288

commit v2 on v1

--- a/solution.py
+++ b/solution.py
@@ -14,12 +14,12 @@
 LOW_FREQUENCY = 5.0
 FREQUENCY_BAND = 50.0
 DAMPING = 6.0
-X_RADIX = 8
 LANES = 128
 LAG = 2
-DEPTH = 4
+BEHIND = 3
+SKIP = 2
+OWN = 4
 YTALL = 64
-EARLY = 2
 MESH = pl.DeviceIdType.MESH
 
 HALF_SIN = (0.9999998807907104, -0.16666465997695923, 0.008326363749802113, -0.00019062065985053778)
@@ -90,8 +90,8 @@
 def kernel(
     groups, radix, pieces, freq_total,
     wavelet, freq_index, slowness, layer_ids, rays, spec_hbm, out_ref,
-    spec, zed, ytab, field, xtab, vecs, fac, image, core_in, pair_in, low_in, high_in, etile, eall,
-    load_sem, core_s, core_r, pair_s, pair_r, low_s, low_r, high_s, high_r, e_s, e_r,
+    spec, zed, ytab, field, xtab, yout, fac, image, core_in, pair_in, low_in, high_in, other_in, etile, eall,
+    load_sem, core_s, core_r, pair_s, pair_r, low_s, low_r, high_s, high_r, other_s, other_r, e_s, e_r,
 ):
     rows = spec.shape[1] * spec.shape[2]
     cols = spec.shape[3]
@@ -144,35 +144,26 @@
     wave_re = wavelet[0, 0]
     wave_im = wavelet[0, 1]
 
-    block = cols // X_RADIX
-    place = lax.broadcasted_iota(jnp.int32, (X_RADIX, cols), 1)
-    outer = lax.broadcasted_iota(jnp.int32, (X_RADIX, cols), 0)
-    eighth = lax.rem(place * outer, X_RADIX).astype(jnp.float32) * (1.0 / X_RADIX)
-    vec_sin, vec_cos = turn_sincos(eighth + place.astype(jnp.float32) * turn_x)
-    vecs[0] = vec_cos
-    vecs[1] = vec_sin
-
     width = cols // pieces
     deep = 32
 
     def x_table(p):
-        at = pl.ds(pl.multiple_of(p * width, LANES), width)
-        x = lax.broadcasted_iota(jnp.int32, (deep, width), 1) + p * width
-        x = x.astype(jnp.float32) * (1.0 / cols)
+        x = lax.broadcasted_iota(jnp.int32, (deep, width), 1) * pieces + p
+        x = x.astype(jnp.float32)
+        away = x * turn_x
+        away = away - jnp.floor(away)
+        x = x * (1.0 / cols)
         k = lax.broadcasted_iota(jnp.int32, (deep, width), 0)
 
         def strip_of(strip, carry):
-            sine, cosine = turn_sincos((k + strip * deep).astype(jnp.float32) * x)
-            for k1 in range(X_RADIX):
-                vc = vecs[0, k1 : k1 + 1, at]
-                vs = vecs[1, k1 : k1 + 1, at]
-                row = pl.ds(pl.multiple_of(strip * deep + k1 * block, deep), deep)
-                row_im = pl.ds(pl.multiple_of(strip * deep + k1 * block + cols, deep), deep)
-                xtab[row, at] = (cosine * vc - sine * vs).astype(jnp.bfloat16)
-                xtab[row_im, at] = (-(cosine * vs) - sine * vc).astype(jnp.bfloat16)
+            sine, cosine = turn_sincos((k + strip * deep).astype(jnp.float32) * x + away)
+            row = pl.ds(pl.multiple_of(strip * deep, deep), deep)
+            row_im = pl.ds(pl.multiple_of(strip * deep + width, deep), deep)
+            xtab[p, row, :] = cosine.astype(jnp.bfloat16)
+            xtab[p, row_im, :] = (-sine).astype(jnp.bfloat16)
             return carry
 
-        lax.fori_loop(0, block // deep, strip_of, 0, unroll=True)
+        lax.fori_loop(0, width // deep, strip_of, 0, unroll=True)
 
     with scope("xt0"):
         x_table(0)
@@ -263,7 +254,7 @@
         return carry
 
     with scope("factors"):
-        lax.fori_loop(0, rows // 16, factors, 0)
+        lax.fori_loop(0, rows // 16, factors, 0, unroll=4)
 
     def shift(strip, total):
         load(strip).wait()
@@ -297,13 +288,23 @@
     chips = groups // 2
 
     def y_stage(n1, carry):
-        for part in range(cols // 256):
-            at = slice(part * 256, part * 256 + 256)
-            at_im = slice(cols + part * 256, cols + part * 256 + 256)
-            res = jnp.dot(ytab[n1], zed[n1, :, at], preferred_element_type=jnp.float32)
-            res = res.astype(jnp.bfloat16)
-            field[:, n1, :, at] = res[:short].reshape(chips, 16, 256)
-            field[:, n1, :, at_im] = res[short:].reshape(chips, 16, 256)
+        for part in range(pieces):
+            at = slice(part * width, (part + 1) * width)
+            yout[part] = jnp.dot(ytab[n1], zed[n1, :, at], preferred_element_type=jnp.float32)
+
+        def fold(strip, inner):
+            top = pl.ds(pl.multiple_of(strip * 16, 16), 16)
+            low = pl.ds(pl.multiple_of(strip * 16 + short, 16), 16)
+            for lane_tile in range(width // LANES):
+                left = slice(lane_tile * LANES, (lane_tile + 1) * LANES)
+                right = slice(width + lane_tile * LANES, width + (lane_tile + 1) * LANES)
+                terms = [(yout[part, top, left], yout[part, low, left]) for part in range(pieces)]
+                for x1, (re, im) in enumerate(butterfly(terms)):
+                    field[x1, strip, n1, :, left] = re.astype(jnp.bfloat16)
+                    field[x1, strip, n1, :, right] = im.astype(jnp.bfloat16)
+            return inner
+
+        lax.fori_loop(0, chips, fold, 0, unroll=True)
         return carry
 
     with scope("ystage"):
@@ -324,18 +325,52 @@
 
     lax.fori_loop(1, groups, energy_start, 0)
 
-    def order(j):
-        half = j // 2
-        return jnp.where(lax.rem(j, 2) == 0, half, lines - 1 - half)
+    def ranked(j, count, centre):
+        up = count - 1 - centre
+        near = jnp.minimum(up, centre)
+        lead = jnp.maximum(up, centre) - near
+        sign = jnp.where(up >= centre, 1, -1)
+        rest = jnp.maximum(j - lead, 0)
+        side = jnp.where(lax.rem(rest, 2) == 0, sign, -sign)
+        return jnp.where(j < lead, centre + sign * (lead + near - j), centre + side * (near - rest // 2))
+
+    half = max(lines // 4, 1)
+    blocks = lines // half
+    away = (lines - 1) * pieces
+
+    def piece(i):
+        up = lines - 1 - spot
+        near = jnp.minimum(up, spot)
+        lead = jnp.maximum(up, spot) - near
+        sign = jnp.where(up >= spot, 1, -1)
+        rest = jnp.maximum(i - lead * pieces, 0)
+        turn = lax.rem(rest, 2 * pieces)
+        side = jnp.where(lax.rem(turn, 2) == 0, -sign, sign)
+        single = i < lead * pieces
+        a = jnp.where(
+            single,
+            spot + sign * (lead + near - i // pieces),
+            spot + side * (near - rest // (2 * pieces)),
+        )
+        p = jnp.where(single, lax.rem(i, pieces), turn // 2)
+        own = i >= away
+        return jnp.where(own, spot, a), jnp.where(own, i - away, p)
+
+    def unpaired(sender, a, p):
+        beside = (a == sender + 1) | (a == sender - 1)
+        inner = (a == 0) | (a == lines - 1)
+        outer = ((sender == 0) | (sender == lines - 1)) & (p < SKIP)
+        return beside & (inner | outer)
 
     def cut_of(p):
         return pl.ds(pl.multiple_of(p * width, LANES), width)
 
-    def core_copy(p, b):
-        cut = cut_of(p)
+    def core_copy(block, p, b):
+        cut = cut_of(p)
+        at = pl.ds(block * half, half)
         return pltpu.make_async_remote_copy(
-            src_ref=image.at[:, b, 1 - core, :, :, cut], dst_ref=core_in.at[:, b, :, :, cut],
-            send_sem=core_s.at[p, b], recv_sem=core_r.at[p, b],
+            src_ref=image.at[at, b, 1 - core, :, :, cut], dst_ref=core_in.at[at, b, :, :, cut],
+            send_sem=core_s.at[block, p, b], recv_sem=core_r.at[block, p, b],
             device_id={"freq": core_peer}, device_id_type=MESH,
         )
 
@@ -365,106 +400,142 @@
             device_id_type=MESH,
         )
 
-    count = lines * pieces
-    depth = min(DEPTH, count)
-
-    def split(i):
-        return order(lax.rem(i, lines)), i // lines
-
-    def first_of(i):
-        return lax.rem(i, lines) == 0
-
-    def send_pair(i):
-        a, p = split(i)
-        cut = cut_of(p)
-
-        @pl.when(first_of(i))
-        def _():
-            core_copy(p, 1 - pair).wait_recv()
-
-        image[a, 1 - pair, core, :, :, cut] = (
-            image[a, 1 - pair, core, :, :, cut] + core_in[a, 1 - pair, :, :, cut]
-        )
-        pair_copy(a, p).start()
-
-    def third(i, carry):
-        @pl.when(i < count)
-        def _():
-            a, p = split(jnp.minimum(i, count - 1))
+    def other_copy(upward, p):
+        cut = cut_of(p)
+        step = 1 if upward else -1
+        return pltpu.make_async_remote_copy(
+            src_ref=image.at[jnp.clip(spot + step, 0, lines - 1), 1 - pair, core, :, :, cut],
+            dst_ref=other_in.at[0 if upward else 1, :, :, cut],
+            send_sem=other_s.at[0 if upward else 1, p], recv_sem=other_r.at[0 if upward else 1, p],
+            device_id={"freq": jnp.clip(spot + step, 0, lines - 1) * 4 + pair * 2 + core},
+            device_id_type=MESH,
+        )
+
+    def block_of(c):
+        if half == 1:
+            return piece(c)
+        return ranked(c // pieces, blocks, spot // half), lax.rem(c, pieces)
+
+    def take_core(c):
+        block, p = block_of(c)
+        at = pl.ds(block * half, half)
+        cut = cut_of(p)
+        with scope("cw1"):
+            core_copy(block, p, 1 - pair).wait_recv()
+        image[at, 1 - pair, core, :, :, cut] = (
+            image[at, 1 - pair, core, :, :, cut] + core_in[at, 1 - pair, :, :, cut]
+        )
+        for h in range(half):
+            a = block * half + h
+            skipped = unpaired(spot, a, p)
+
+            @pl.when(jnp.logical_not(skipped) & (a != spot))
+            def _():
+                pair_copy(a, p).start()
+
+            @pl.when(skipped & (a > spot))
+            def _():
+                other_copy(True, p).start()
+
+            @pl.when(skipped & (a < spot))
+            def _():
+                other_copy(False, p).start()
+
+        with scope("cw2"):
+            core_copy(block, p, pair).wait_recv()
+        image[at, pair, core, :, :, cut] = image[at, pair, core, :, :, cut] + core_in[at, pair, :, :, cut]
+
+    def own_start(p):
+        cut = cut_of(p)
+
+        @pl.when((spot > 0) & unpaired(spot - 1, spot, p))
+        def _():
+            with scope("ow"):
+                other_copy(True, p).wait_recv()
+            image[spot, 1 - pair, core, :, :, cut] = image[spot, 1 - pair, core, :, :, cut] + other_in[0, :, :, cut]
+
+        @pl.when((spot < lines - 1) & unpaired(spot + 1, spot, p))
+        def _():
+            with scope("ow"):
+                other_copy(False, p).wait_recv()
+            image[spot, 1 - pair, core, :, :, cut] = image[spot, 1 - pair, core, :, :, cut] + other_in[1, :, :, cut]
+
+        pair_copy(spot, p).start()
+
+    lag = LAG * jnp.minimum(spot, lines - 1 - spot)
+
+    def step(i, carry):
+        a, p = piece(jnp.minimum(i, away - 1))
+
+        @pl.when((i < away) & jnp.logical_not(unpaired(spot, a, p)))
+        def _():
             cut = cut_of(p)
-            pair_copy(a, p).wait_recv()
-
-            @pl.when(i + depth < count)
-            def _():
-                send_pair(jnp.minimum(i + depth, count - 1))
-
-            @pl.when(first_of(i))
-            def _():
-                core_copy(p, pair).wait_recv()
-
-            image[a, pair, core, :, :, cut] = (
-                image[a, pair, core, :, :, cut] + core_in[a, pair, :, :, cut] + pair_in[a, :, :, cut]
-            )
-
-        upward = i - LAG * spot
-        a_up, p_up = split(jnp.clip(upward, 0, count - 1))
-
-        @pl.when((upward >= 0) & (upward < count) & (a_up > spot))
-        def _():
-            cut = cut_of(p_up)
-
-            @pl.when(spot > 0)
-            def _():
-                low_copy(a_up, p_up).wait_recv()
-                image[a_up, pair, core, :, :, cut] = image[a_up, pair, core, :, :, cut] + low_in[a_up, :, :, cut]
-
-            low_copy(a_up, p_up).start()
-
-        downward = i - LAG * (lines - 1 - spot)
-        a_dn, p_dn = split(jnp.clip(downward, 0, count - 1))
-
-        @pl.when((downward >= 0) & (downward < count) & (a_dn < spot))
-        def _():
-            cut = cut_of(p_dn)
-
-            @pl.when(spot < lines - 1)
-            def _():
-                high_copy(a_dn, p_dn).wait_recv()
-                image[a_dn, pair, core, :, :, cut] = image[a_dn, pair, core, :, :, cut] + high_in[a_dn, :, :, cut]
-
-            high_copy(a_dn, p_dn).start()
-
-        return carry
-
-    def compute(p, carry):
+            with scope("yw"):
+                pair_copy(a, p).wait_recv()
+            image[a, pair, core, :, :, cut] = image[a, pair, core, :, :, cut] + pair_in[a, :, :, cut]
+
+        @pl.when(i >= lag)
+        def _():
+            a, p = piece(jnp.clip(i - lag, 0, away - 1))
+            cut = cut_of(p)
+
+            @pl.when(a > spot)
+            def _():
+                @pl.when(spot > 0)
+                def _():
+                    with scope("zw"):
+                        low_copy(a, p).wait_recv()
+                    image[a, pair, core, :, :, cut] = image[a, pair, core, :, :, cut] + low_in[a, :, :, cut]
+
+                low_copy(a, p).start()
+
+            @pl.when(a < spot)
+            def _():
+                @pl.when(spot < lines - 1)
+                def _():
+                    with scope("zw"):
+                        high_copy(a, p).wait_recv()
+                    image[a, pair, core, :, :, cut] = image[a, pair, core, :, :, cut] + high_in[a, :, :, cut]
+
+                high_copy(a, p).start()
+
+        @pl.when((i >= OWN) & (i < OWN + pieces))
+        def _():
+            own_start(i - OWN)
+
+        return carry
+
+    chunks = blocks * pieces
+
+    def compute(c, carry):
+        block, p = block_of(c)
         at = cut_of(p)
 
-        @pl.when(p > 0)
+        @pl.when((c > 0) & (c < pieces))
         def _():
             x_table(p)
 
-        @pl.when(p == 1)
-        def _():
-            lax.fori_loop(0, depth, lambda i, c: (send_pair(i), c)[1], 0)
-
-        lax.fori_loop(EARLY * jnp.maximum(p - 2, 0), EARLY * jnp.maximum(p - 1, 0), third, 0)
-
-        half = max(lines // 4, 1)
-        for q in range(lines // half):
-            lhs = field[2 * half * q : 2 * half * (q + 1)].reshape(half * 2 * radix * 16, 2 * cols)
-            res = jnp.dot(lhs, xtab[:, at], preferred_element_type=jnp.float32)
+        with scope("dot"):
+            lhs = field[p, pl.ds(2 * half * block, 2 * half)].reshape(half * 2 * radix * 16, 2 * width)
+            res = jnp.dot(lhs, xtab[p], preferred_element_type=jnp.float32)
             res = res.reshape(half, 2, radix, 2, 8, width)
-            for c in range(2):
-                image[half * q : half * (q + 1), :, c, :, :, at] = res[:, :, :, c]
-        core_copy(p, 1 - pair).start()
-        core_copy(p, pair).start()
+            for c_ in range(2):
+                image[pl.ds(half * block, half), :, c_, :, :, at] = res[:, :, :, c_]
+        core_copy(block, p, 1 - pair).start()
+        core_copy(block, p, pair).start()
+
+        @pl.when(c >= BEHIND)
+        def _():
+            take_core(c - BEHIND)
+
         return carry
 
     with scope("compute"):
-        lax.fori_loop(0, pieces, compute, 0)
+        lax.fori_loop(0, chunks, compute, 0)
+        lax.fori_loop(chunks - BEHIND, chunks, lambda c, carry: (take_core(c), carry)[1], 0)
 
     with scope("third"):
-        lax.fori_loop(EARLY * max(pieces - 2, 0), count + LAG * (lines - 1), third, 0)
+        lax.fori_loop(0, away + lag, step, 0)
 
     def energy_take(i, total):
         energy_copy(i).wait_recv()
@@ -474,25 +545,39 @@
     total = jnp.sum(jnp.sum(total, axis=0, keepdims=True), axis=1, keepdims=True)
     scale = lax.rsqrt(total / freq_total + 1e-06)
 
+    lanes8 = lax.broadcasted_iota(jnp.int32, (8, LANES), 1)
+    part_lane = lanes8 // pieces
+    lane_part = lax.rem(lanes8, pieces)
+
     def own(p, carry):
         cut = cut_of(p)
+        with scope("oyw"):
+            pair_copy(spot, p).wait_recv()
+        image[spot, pair, core, :, :, cut] = image[spot, pair, core, :, :, cut] + pair_in[spot, :, :, cut]
 
         @pl.when(spot > 0)
         def _():
-            low_copy(spot, p).wait_recv()
+            with scope("ozw"):
+                low_copy(spot, p).wait_recv()
             image[spot, pair, core, :, :, cut] = image[spot, pair, core, :, :, cut] + low_in[spot, :, :, cut]
 
         @pl.when(spot < lines - 1)
         def _():
-            high_copy(spot, p).wait_recv()
+            with scope("ozw"):
+                high_copy(spot, p).wait_recv()
             image[spot, pair, core, :, :, cut] = image[spot, pair, core, :, :, cut] + high_in[spot, :, :, cut]
 
+        for n1 in range(radix):
+            for j in range(tiles):
+                source = pl.ds(pl.multiple_of(p * width + j // pieces * LANES, LANES), LANES)
+                value = image[spot, pair, core, n1, :, source] * scale
+                spread = jnp.take_along_axis(value, part_lane + j % pieces * (LANES // pieces), axis=1)
+                to = slice(j * LANES, (j + 1) * LANES)
+                out_ref[:, n1, to] = jnp.where(lane_part == p, spread, out_ref[:, n1, to])
         return carry
 
     with scope("own"):
         lax.fori_loop(0, pieces, own, 0)
-    for n1 in range(radix):
-        out_ref[:, n1, :] = image[spot, pair, core, n1] * scale
 
     def energy_end(i, carry):
         energy_copy(i).wait_send()
@@ -500,16 +585,29 @@
 
     lax.fori_loop(1, groups, energy_end, 0)
 
-    def finish_core(p, carry):
-        core_copy(p, 0).wait_send()
-        core_copy(p, 1).wait_send()
-        return carry
-
-    lax.fori_loop(0, pieces, finish_core, 0)
+    def finish_core(block, carry):
+        def ended(p, inner):
+            core_copy(block, p, 0).wait_send()
+            core_copy(block, p, 1).wait_send()
+            return inner
+
+        return lax.fori_loop(0, pieces, ended, carry)
+
+    lax.fori_loop(0, blocks, finish_core, 0)
 
     def finish(a, carry):
-        def piece(p, inner):
-            pair_copy(a, p).wait_send()
+        def ended(p, inner):
+            @pl.when(jnp.logical_not(unpaired(spot, a, p)))
+            def _():
+                pair_copy(a, p).wait_send()
+
+            @pl.when(unpaired(spot, a, p) & (a > spot))
+            def _():
+                other_copy(True, p).wait_send()
+
+            @pl.when(unpaired(spot, a, p) & (a < spot))
+            def _():
+                other_copy(False, p).wait_send()
 
             @pl.when(a > spot)
             def _():
@@ -521,7 +619,7 @@
 
             return inner
 
-        return lax.fori_loop(0, pieces, piece, carry)
+        return lax.fori_loop(0, pieces, ended, carry)
 
     lax.fori_loop(0, lines, finish, 0)
 
@@ -548,26 +646,29 @@
             pltpu.VMEM((2, radix, short, cols), bf16),
             pltpu.VMEM((radix, 2 * short, cols), bf16),
             pltpu.VMEM((radix, 2 * short, 2 * short), bf16),
-            pltpu.VMEM((groups // 2, radix, 16, 2 * cols), bf16),
-            pltpu.VMEM((2 * cols, cols), bf16),
-            pltpu.VMEM((2, X_RADIX, cols), f32),
+            pltpu.VMEM((pieces, groups // 2, radix, 16, 2 * (cols // pieces)), bf16),
+            pltpu.VMEM((pieces, 2 * (cols // pieces), cols // pieces), bf16),
+            pltpu.VMEM((pieces, 2 * short, cols // pieces), f32),
             pltpu.VMEM((2, rows, cols), f32),
             pltpu.VMEM((lines, 2, 2, radix, 8, cols), f32),
             pltpu.VMEM((lines, 2, radix, 8, cols), f32),
             pltpu.VMEM((lines, radix, 8, cols), f32),
             pltpu.VMEM((lines, radix, 8, cols), f32),
             pltpu.VMEM((lines, radix, 8, cols), f32),
+            pltpu.VMEM((2, radix, 8, cols), f32),
             pltpu.VMEM((8, LANES), f32),
             pltpu.VMEM((groups, 8, LANES), f32),
             dma((short // 16,)),
-            dma((pieces, 2)),
-            dma((pieces, 2)),
+            dma((min(lines, 4), pieces, 2)),
+            dma((min(lines, 4), pieces, 2)),
             dma((lines, pieces)),
             dma((lines, pieces)),
             dma((lines, pieces)),
             dma((lines, pieces)),
             dma((lines, pieces)),
             dma((lines, pieces)),
+            dma((2, pieces)),
+            dma((2, pieces)),
             dma((groups,)),
             dma((groups,)),
         ],

time: 57.8 us -> 45.1 us (0.78)
  the two profiles are of different devices: /device:TPU:0 before, /device:TPU:19 now
where the time goes in v2:
time: 45.1 us; the launch traced here: 44.9 us
  Pallas kernels  42 us (93%)
  local copies, waits for them, and re-layouts  1.67 us (4%)
  between operations  1.3 us (3%)
    pallas_call x1, Pallas kernels, body(): pl.pallas_call(functools.partial(kernel, groups, radix, pieces, freq_tota...  42 us
    unnamed x1, local copies, waits for them, and re-layouts  1.67 us

profile of v2, /device:TPU:19, one launch (start us, length us, event | category | flops | bytes accessed | tf_op | source)
XLA Modules:
  0.0 44.9 jit_solution(5313121216928214169)
XLA Ops:
  1.3 42.0 %shard_map.64 = f32[8,8,1024]{2,1,0:T(8,128)} custom-call(f32[1,2]{1,0:T(1,128)} %wavelet.1, s32[1,1]{1,0:T(1,128)} %bitcast.4.freq_index, f32[16]{0:T(128)} %slowness.1, s32[1,1]{1,0:T(1,128)} %bitcast.5.layer_ids, f32[2]{0:T(128)} %rays.1, bf16[2,8,128,1024]{3,2,1,0:T(8,128)(2,1)} %bitcast.6), custom_call_target="tpu_custom_call" | custom-call | tf_op jit(solution)/shard_map/pallas_call | solution.py:637
  43.3 1.7 %copy.10 = f32[1,64,1024]{2,1,0:T(8,128)} copy(f32[1,64,1024]{2,1,0:T(8,128)} %bitcast.7) | data formatting | bytes 524288

commit v3 on v2

--- a/solution.py
+++ b/solution.py
@@ -18,6 +18,9 @@
 LAG = 2
 BEHIND = 3
 SKIP = 2
+FIRST = 2
+HEAD = 1
+EARLY = (11, 14)
 OWN = 4
 YTALL = 64
 MESH = pl.DeviceIdType.MESH
@@ -91,7 +94,7 @@
     groups, radix, pieces, freq_total,
     wavelet, freq_index, slowness, layer_ids, rays, spec_hbm, out_ref,
     spec, zed, ytab, field, xtab, yout, fac, image, core_in, pair_in, low_in, high_in, other_in, etile, eall,
-    load_sem, core_s, core_r, pair_s, pair_r, low_s, low_r, high_s, high_r, other_s, other_r, e_s, e_r,
+    load_sem, core_s, core_r, pair_s, pair_r, line_s, line_r, other_r, e_s, e_r,
 ):
     rows = spec.shape[1] * spec.shape[2]
     cols = spec.shape[3]
@@ -106,13 +109,17 @@
 
     barrier = pltpu.get_barrier_semaphore()
 
+    with scope("begin"):
+        core_peer = core_peer + 0
+
     def greet(i, carry):
         pl.semaphore_signal(
             barrier, inc=1, device_id={"freq": lax.rem(me + i, groups)}, device_id_type=MESH
         )
         return carry
 
-    lax.fori_loop(1, groups, greet, 0)
+    with scope("greet"):
+        lax.fori_loop(1, groups, greet, 0)
 
     strips = short // 16
     tiles = cols // LANES
@@ -120,14 +127,15 @@
     def load(i):
         window = pl.ds(pl.multiple_of(i * 16, 16), 16)
         return pltpu.make_async_copy(
-            spec_hbm.at[:, :, window, :], spec.at[:, :, window, :], load_sem.at[i]
+            spec_hbm.at[:, :, window, :], spec.at[:, :, window, :], load_sem
         )
 
     def start_load(i, carry):
         load(i).start()
         return carry
 
-    lax.fori_loop(0, strips, start_load, 0)
+    with scope("loads"):
+        lax.fori_loop(0, strips, start_load, 0)
 
     hertz = freq_index[0, 0].astype(jnp.float32) * (FREQUENCY_BAND / freq_total) + LOW_FREQUENCY
     angular = hertz * (2.0 * math.pi)
@@ -225,39 +233,58 @@
     def signed(index, extent):
         return jnp.where(index >= extent // 2, index - extent, index).astype(jnp.float32)
 
-    lane = lax.broadcasted_iota(jnp.int32, (16, LANES), 1)
-    sub = lax.broadcasted_iota(jnp.int32, (16, LANES), 0)
+    lane = lax.broadcasted_iota(jnp.int32, (8, LANES), 1)
+    sub = lax.broadcasted_iota(jnp.int32, (8, LANES), 0)
     kx_sq = []
     for t in range(tiles // 2):
         kx = (lane + t * LANES).astype(jnp.float32) * step_x
         kx_sq.append(kx * kx)
-    edge_y = signed(lane * 16 + sub, rows) * step_y
     edge_x = cols // 2 * step_x
+    turned = lax.rem(LANES - lane, LANES)
+    flipped = lax.rem(8 - sub, 8)
+    first = lane == 0
+    top = sub == 0
+    edge_y = (lane * 8 + sub).astype(jnp.float32) * step_y
     edge = factor(base - edge_x * edge_x - edge_y * edge_y)
-    turned = lax.rem(LANES - lane, LANES)
-    first = lane == 0
-
-    def factors(m, carry):
-        rows_at = pl.ds(pl.multiple_of(m * 16, 16), 16)
-        ky = signed(sub + m * 16, rows) * step_y
+
+    def factor_rows(m, put):
+        ky = (sub + m * 8).astype(jnp.float32) * step_y
         ybase = base - ky * ky
-        here = jnp.full((16, LANES), m, jnp.int32)
+        here = jnp.full((8, LANES), m, jnp.int32)
         after = [jnp.take_along_axis(e, here, axis=1) for e in edge]
         for t in reversed(range(tiles // 2)):
             now = factor(ybase - kx_sq[t])
             for c in range(2):
-                fac[c, rows_at, t * LANES : (t + 1) * LANES] = now[c]
+                put(c, t, now[c])
                 back = jnp.take_along_axis(now[c], turned, axis=1)
-                far = tiles - 1 - t
-                fac[c, rows_at, far * LANES : (far + 1) * LANES] = jnp.where(first, after[c], back)
+                put(c, tiles - 1 - t, jnp.where(first, after[c], back))
             after = now
-        return carry
+
+    middle = {}
+
+    def put_middle(c, t, value):
+        middle[c, t] = value
+
+    def factors(i, carry):
+        m = rows // 16 - 1 - i
+        here = pl.ds(pl.multiple_of(m * 8, 8), 8)
+        values = {}
+        low = pl.ds(pl.multiple_of(rows - 8 - m * 8, 8), 8)
+
+        def put(c, t, value):
+            at = slice(t * LANES, (t + 1) * LANES)
+            fac[c, low, at] = jnp.where(top, carry[c, t], jnp.take_along_axis(value, flipped, axis=0))
+            fac[c, here, at] = value
+            values[c, t] = value
+
+        factor_rows(m, put)
+        return values
 
     with scope("factors"):
-        lax.fori_loop(0, rows // 16, factors, 0, unroll=4)
+        factor_rows(rows // 16, put_middle)
+        lax.fori_loop(0, rows // 16, factors, middle, unroll=8)
 
     def shift(strip, total):
-        load(strip).wait()
         rows_at = pl.ds(pl.multiple_of(strip * 16, 16), 16)
 
         def inner(tile, acc):
@@ -279,9 +306,10 @@
                 zed[n1, low, at] = im
             return acc
 
-        return lax.fori_loop(0, tiles, inner, total, unroll=2)
+        return lax.fori_loop(0, tiles, inner, total, unroll=8)
 
     with scope("shift"):
+        pltpu.make_async_copy(spec_hbm, spec, load_sem).wait()
         energy = lax.fori_loop(0, strips, shift, jnp.zeros((16, LANES), jnp.float32))
     etile[...] = energy[:8] + energy[8:]
 
@@ -315,7 +343,7 @@
 
     def energy_copy(i):
         return pltpu.make_async_remote_copy(
-            src_ref=etile, dst_ref=eall.at[i], send_sem=e_s.at[i], recv_sem=e_r.at[i],
+            src_ref=etile, dst_ref=eall.at[i], send_sem=e_s, recv_sem=e_r,
             device_id={"freq": lax.rem(me + i, groups)}, device_id_type=MESH,
         )
 
@@ -365,12 +393,12 @@
     def cut_of(p):
         return pl.ds(pl.multiple_of(p * width, LANES), width)
 
-    def core_copy(block, p, b):
+    def core_copy(block, p):
         cut = cut_of(p)
         at = pl.ds(block * half, half)
         return pltpu.make_async_remote_copy(
-            src_ref=image.at[at, b, 1 - core, :, :, cut], dst_ref=core_in.at[at, b, :, :, cut],
-            send_sem=core_s.at[block, p, b], recv_sem=core_r.at[block, p, b],
+            src_ref=image.at[at, :, 1 - core, :, :, cut], dst_ref=core_in.at[at, :, :, :, cut],
+            send_sem=core_s, recv_sem=core_r.at[block, p],
             device_id={"freq": core_peer}, device_id_type=MESH,
         )
 
@@ -378,7 +406,7 @@
         cut = cut_of(p)
         return pltpu.make_async_remote_copy(
             src_ref=image.at[a, 1 - pair, core, :, :, cut], dst_ref=pair_in.at[a, :, :, cut],
-            send_sem=pair_s.at[a, p], recv_sem=pair_r.at[a, p],
+            send_sem=pair_s, recv_sem=pair_r.at[a, p],
             device_id={"freq": pair_peer}, device_id_type=MESH,
         )
 
@@ -386,16 +414,16 @@
         cut = cut_of(p)
         return pltpu.make_async_remote_copy(
             src_ref=image.at[a, pair, core, :, :, cut], dst_ref=low_in.at[a, :, :, cut],
-            send_sem=low_s.at[a, p], recv_sem=low_r.at[a, p],
+            send_sem=line_s, recv_sem=line_r.at[a, p],
             device_id={"freq": jnp.minimum(spot + 1, lines - 1) * 4 + pair * 2 + core},
             device_id_type=MESH,
         )
 
-    def high_copy(a, p):
+    def high_copy(a, p, arriving=False):
         cut = cut_of(p)
         return pltpu.make_async_remote_copy(
             src_ref=image.at[a, pair, core, :, :, cut], dst_ref=high_in.at[a, :, :, cut],
-            send_sem=high_s.at[a, p], recv_sem=high_r.at[a, p],
+            send_sem=line_s, recv_sem=line_r.at[jnp.where(a == (spot if arriving else spot - 1), lines, a), p],
             device_id={"freq": jnp.maximum(spot - 1, 0) * 4 + pair * 2 + core},
             device_id_type=MESH,
         )
@@ -406,22 +434,29 @@
         return pltpu.make_async_remote_copy(
             src_ref=image.at[jnp.clip(spot + step, 0, lines - 1), 1 - pair, core, :, :, cut],
             dst_ref=other_in.at[0 if upward else 1, :, :, cut],
-            send_sem=other_s.at[0 if upward else 1, p], recv_sem=other_r.at[0 if upward else 1, p],
+            send_sem=pair_s, recv_sem=other_r.at[0 if upward else 1, p],
             device_id={"freq": jnp.clip(spot + step, 0, lines - 1) * 4 + pair * 2 + core},
             device_id_type=MESH,
         )
 
+    ends = (spot == 0) | (spot == lines - 1)
+
     def block_of(c):
         if half == 1:
-            return piece(c)
+            near = (lines - 2) * pieces
+            moved = jnp.where(c < FIRST + SKIP, near + c - FIRST, c - SKIP)
+            return piece(jnp.where(ends & (c >= FIRST) & (c < near + SKIP), moved, c))
         return ranked(c // pieces, blocks, spot // half), lax.rem(c, pieces)
+
+    def hasty(a, p):
+        return unpaired(spot, a, p) & (p < HEAD)
 
     def take_core(c):
         block, p = block_of(c)
         at = pl.ds(block * half, half)
         cut = cut_of(p)
         with scope("cw1"):
-            core_copy(block, p, 1 - pair).wait_recv()
+            core_copy(block, p).wait_recv()
         image[at, 1 - pair, core, :, :, cut] = (
             image[at, 1 - pair, core, :, :, cut] + core_in[at, 1 - pair, :, :, cut]
         )
@@ -441,9 +476,17 @@
             def _():
                 other_copy(False, p).start()
 
-        with scope("cw2"):
-            core_copy(block, p, pair).wait_recv()
         image[at, pair, core, :, :, cut] = image[at, pair, core, :, :, cut] + core_in[at, pair, :, :, cut]
+        for h in range(half):
+            a = block * half + h
+
+            @pl.when((spot == 0) & hasty(a, p))
+            def _():
+                low_copy(a, p).start()
+
+            @pl.when((spot == lines - 1) & hasty(a, p))
+            def _():
+                high_copy(a, p).start()
 
     def own_start(p):
         cut = cut_of(p)
@@ -479,7 +522,7 @@
             a, p = piece(jnp.clip(i - lag, 0, away - 1))
             cut = cut_of(p)
 
-            @pl.when(a > spot)
+            @pl.when((a > spot) & jnp.logical_not((spot == 0) & hasty(a, p)))
             def _():
                 @pl.when(spot > 0)
                 def _():
@@ -489,12 +532,12 @@
 
                 low_copy(a, p).start()
 
-            @pl.when(a < spot)
+            @pl.when((a < spot) & jnp.logical_not((spot == lines - 1) & hasty(a, p)))
             def _():
                 @pl.when(spot < lines - 1)
                 def _():
                     with scope("zw"):
-                        high_copy(a, p).wait_recv()
+                        high_copy(a, p, True).wait_recv()
                     image[a, pair, core, :, :, cut] = image[a, pair, core, :, :, cut] + high_in[a, :, :, cut]
 
                 high_copy(a, p).start()
@@ -510,10 +553,6 @@
     def compute(c, carry):
         block, p = block_of(c)
         at = cut_of(p)
-
-        @pl.when((c > 0) & (c < pieces))
-        def _():
-            x_table(p)
 
         with scope("dot"):
             lhs = field[p, pl.ds(2 * half * block, 2 * half)].reshape(half * 2 * radix * 16, 2 * width)
@@ -521,12 +560,22 @@
             res = res.reshape(half, 2, radix, 2, 8, width)
             for c_ in range(2):
                 image[pl.ds(half * block, half), :, c_, :, :, at] = res[:, :, :, c_]
-        core_copy(block, p, 1 - pair).start()
-        core_copy(block, p, pair).start()
-
-        @pl.when(c >= BEHIND)
+        core_copy(block, p).start()
+
+        @pl.when(c == 0)
+        def _():
+            with scope("xt"):
+                lax.fori_loop(1, pieces, lambda p, carry: (x_table(p), carry)[1], 0)
+            take_core(c)
+
+        @pl.when(c > BEHIND)
         def _():
             take_core(c - BEHIND)
+
+        for i, at_chunk in enumerate(EARLY):
+            @pl.when(c == min(at_chunk, chunks - 1))
+            def _():
+                step(i, 0)
 
         return carry
 
@@ -535,15 +584,25 @@
         lax.fori_loop(chunks - BEHIND, chunks, lambda c, carry: (take_core(c), carry)[1], 0)
 
     with scope("third"):
-        lax.fori_loop(0, away + lag, step, 0)
+        lax.fori_loop(len(EARLY), away + lag, step, 0)
+
+    def all_sent(sem, ref):
+        pltpu.make_async_remote_copy(
+            src_ref=ref, dst_ref=ref, send_sem=sem, recv_sem=sem,
+            device_id={"freq": core_peer}, device_id_type=MESH,
+        ).wait_send()
+
+    all_sent(e_r, eall.at[1:groups])
 
     def energy_take(i, total):
-        energy_copy(i).wait_recv()
         return total + eall[i]
 
     total = lax.fori_loop(1, groups, energy_take, etile[...])
     total = jnp.sum(jnp.sum(total, axis=0, keepdims=True), axis=1, keepdims=True)
     scale = lax.rsqrt(total / freq_total + 1e-06)
+
+    all_sent(e_s, eall.at[1:groups])
+    all_sent(core_s, core_in)
 
     lanes8 = lax.broadcasted_iota(jnp.int32, (8, LANES), 1)
     part_lane = lanes8 // pieces
@@ -564,7 +623,7 @@
         @pl.when(spot < lines - 1)
         def _():
             with scope("ozw"):
-                high_copy(spot, p).wait_recv()
+                high_copy(spot, p, True).wait_recv()
             image[spot, pair, core, :, :, cut] = image[spot, pair, core, :, :, cut] + high_in[spot, :, :, cut]
 
         for n1 in range(radix):
@@ -579,49 +638,9 @@
     with scope("own"):
         lax.fori_loop(0, pieces, own, 0)
 
-    def energy_end(i, carry):
-        energy_copy(i).wait_send()
-        return carry
-
-    lax.fori_loop(1, groups, energy_end, 0)
-
-    def finish_core(block, carry):
-        def ended(p, inner):
-            core_copy(block, p, 0).wait_send()
-            core_copy(block, p, 1).wait_send()
-            return inner
-
-        return lax.fori_loop(0, pieces, ended, carry)
-
-    lax.fori_loop(0, blocks, finish_core, 0)
-
-    def finish(a, carry):
-        def ended(p, inner):
-            @pl.when(jnp.logical_not(unpaired(spot, a, p)))
-            def _():
-                pair_copy(a, p).wait_send()
-
-            @pl.when(unpaired(spot, a, p) & (a > spot))
-            def _():
-                other_copy(True, p).wait_send()
-
-            @pl.when(unpaired(spot, a, p) & (a < spot))
-            def _():
-                other_copy(False, p).wait_send()
-
-            @pl.when(a > spot)
-            def _():
-                low_copy(a, p).wait_send()
-
-            @pl.when(a < spot)
-            def _():
-                high_copy(a, p).wait_send()
-
-            return inner
-
-        return lax.fori_loop(0, pieces, ended, carry)
-
-    lax.fori_loop(0, lines, finish, 0)
+    with scope("ownend"):
+        all_sent(line_s, pair_in.at[1:lines])
+        all_sent(pair_s, pair_in)
 
 
 def body(spectra, wavelet, freq_index, slowness, layer_ids, ray_slowness):
@@ -636,7 +655,7 @@
     dma = pltpu.SemaphoreType.DMA
     out = pl.pallas_call(
         functools.partial(kernel, groups, radix, pieces, freq_total),
-        out_shape=jax.ShapeDtypeStruct((8, radix, cols), f32),
+        out_shape=pltpu.VMEM((8, radix, cols), f32),
         in_specs=[
             *[pl.BlockSpec(memory_space=pltpu.SMEM)] * 5,
             pl.BlockSpec(memory_space=pl.ANY),
@@ -658,19 +677,16 @@
             pltpu.VMEM((2, radix, 8, cols), f32),
             pltpu.VMEM((8, LANES), f32),
             pltpu.VMEM((groups, 8, LANES), f32),
-            dma((short // 16,)),
-            dma((min(lines, 4), pieces, 2)),
-            dma((min(lines, 4), pieces, 2)),
+            dma,
+            dma,
+            dma((min(lines, 4), pieces)),
+            dma,
             dma((lines, pieces)),
-            dma((lines, pieces)),
-            dma((lines, pieces)),
-            dma((lines, pieces)),
-            dma((lines, pieces)),
-            dma((lines, pieces)),
+            dma,
+            dma((lines + 1, pieces)),
             dma((2, pieces)),
-            dma((2, pieces)),
-            dma((groups,)),
-            dma((groups,)),
+            dma,
+            dma,
         ],
         compiler_params=pltpu.CompilerParams(
             collective_id=0, has_side_effects=True, vmem_limit_bytes=60 * 1024 * 1024

time: 45.1 us -> 38.2 us (0.85)
  the two profiles are of different devices: /device:TPU:19 before, /device:TPU:0 now
where the time goes in v3:
time: 38.2 us; the launch traced here: 37.9 us
  Pallas kernels  35.9 us (94%)
  between operations  1.3 us (3%)
  local copies, waits for them, and re-layouts  0.71 us (2%)
    pallas_call x1, Pallas kernels, body(): pl.pallas_call(functools.partial(kernel, groups, radix, pieces, freq_tota...  35.9 us

profile of v3, /device:TPU:0, one launch (start us, length us, event | category | flops | bytes accessed | tf_op | source)
XLA Modules:
  0.0 37.9 jit_solution(733806557915528231)
XLA Ops:
  1.3 35.9 %shard_map.64 = f32[8,8,1024]{2,1,0:T(8,128)S(1)} custom-call(f32[1,2]{1,0:T(1,128)} %wavelet.1, s32[1,1]{1,0:T(1,128)} %bitcast.4.freq_index, f32[16]{0:T(128)} %slowness.1, s32[1,1]{1,0:T(1,128)} %bitcast.5.layer_ids, f32[2]{0:T(128)} %rays.1, bf16[2,8,128,1024]{3,2,1,0:T(8,128)(2,1)} %bitcast.7), custom_call_target="tpu_custom_call" | custom-call | tf_op jit(solution)/shard_map/pallas_call | solution.py:656
  37.2 0.7 %copy.8 = f32[1,64,1024]{2,1,0:T(8,128)} copy(f32[1,64,1024]{2,1,0:T(8,128)S(1)} %bitcast.6) | data formatting | bytes 524288

commit v4 on v3

--- a/solution.py
+++ b/solution.py
@@ -92,12 +92,13 @@
 
 def kernel(
     groups, radix, pieces, freq_total,
-    wavelet, freq_index, slowness, layer_ids, rays, spec_hbm, out_ref,
-    spec, zed, ytab, field, xtab, yout, fac, image, core_in, pair_in, low_in, high_in, other_in, etile, eall,
-    load_sem, core_s, core_r, pair_s, pair_r, line_s, line_r, other_r, e_s, e_r,
+    wavelet_hbm, freq_hbm, slowness_hbm, layer_hbm, rays_hbm, spec_hbm, out_ref,
+    wavelet, freq_index, slowness, layer_ids, rays,
+    spec, zed, ytab, field, xtab, yout, vecs, xbase, fac, mixed, image, core_in, pair_in, low_in, high_in, other_in, etile, eall,
+    small_sem, load_sem, core_s, core_r, pair_s, pair_r, line_s, line_r, other_r, e_s, e_r,
 ):
     rows = spec.shape[1] * spec.shape[2]
-    cols = spec.shape[3]
+    cols = spec_hbm.shape[3]
     short = rows // radix
     lines = groups // 4
     me = lax.axis_index("freq")
@@ -108,9 +109,26 @@
     pair_peer = me + 2 - 4 * pair
 
     barrier = pltpu.get_barrier_semaphore()
-
-    with scope("begin"):
-        core_peer = core_peer + 0
+    strips = short // 16
+    tiles = cols // LANES
+    small = [
+        pltpu.make_async_copy(source, place, small_sem.at[i])
+        for i, (source, place) in enumerate((
+            (freq_hbm, freq_index), (layer_hbm, layer_ids), (slowness_hbm, slowness),
+            (rays_hbm, rays), (wavelet_hbm, wavelet),
+        ))
+    ]
+    for copy in small:
+        copy.start()
+
+    def start_load(i, carry):
+        window = pl.ds(pl.multiple_of(i * 16, 16), 16)
+        pltpu.make_async_copy(
+            spec_hbm.at[:, :, window, :], spec.at[:, :, window, pl.ds(0, cols)], load_sem
+        ).start()
+        return carry
+
+    lax.fori_loop(0, strips, start_load, 0)
 
     def greet(i, carry):
         pl.semaphore_signal(
@@ -119,27 +137,29 @@
         return carry
 
     with scope("greet"):
-        lax.fori_loop(1, groups, greet, 0)
-
-    strips = short // 16
-    tiles = cols // LANES
-
-    def load(i):
-        window = pl.ds(pl.multiple_of(i * 16, 16), 16)
-        return pltpu.make_async_copy(
-            spec_hbm.at[:, :, window, :], spec.at[:, :, window, :], load_sem
-        )
-
-    def start_load(i, carry):
-        load(i).start()
-        return carry
-
-    with scope("loads"):
-        lax.fori_loop(0, strips, start_load, 0)
-
-    hertz = freq_index[0, 0].astype(jnp.float32) * (FREQUENCY_BAND / freq_total) + LOW_FREQUENCY
+        lax.fori_loop(1, groups, greet, 0, unroll=True)
+
+    width = cols // pieces
+    deep = 32
+
+    def x_base(strip, carry):
+        k = lax.broadcasted_iota(jnp.int32, (deep, width), 0) + strip * deep
+        x2 = lax.broadcasted_iota(jnp.int32, (deep, width), 1)
+        sine, cosine = turn_sincos((k * x2).astype(jnp.float32) * (1.0 / width))
+        row = pl.ds(pl.multiple_of(strip * deep, deep), deep)
+        xbase[0, row, :] = cosine
+        xbase[1, row, :] = sine
+        return carry
+
+    with scope("xbase"):
+        lax.fori_loop(0, width // deep, x_base, 0, unroll=True)
+    with scope("small"):
+        for copy in small:
+            copy.wait()
+
+    hertz = freq_index[0].astype(jnp.float32) * (FREQUENCY_BAND / freq_total) + LOW_FREQUENCY
     angular = hertz * (2.0 * math.pi)
-    slow = slowness[layer_ids[0, 0]]
+    slow = slowness[layer_ids[0]]
     slow_sq = slow * slow
     ray_x = rays[0]
     ray_y = rays[1]
@@ -152,8 +172,14 @@
     wave_re = wavelet[0, 0]
     wave_im = wavelet[0, 1]
 
-    width = cols // pieces
-    deep = 32
+    def x_first(strip, carry):
+        row = pl.ds(pl.multiple_of(strip * deep, deep), deep)
+        row_im = pl.ds(pl.multiple_of(strip * deep + width, deep), deep)
+        cosine = xbase[0, row, :]
+        sine = xbase[1, row, :]
+        xtab[0, row, :] = (cosine * col_cos - sine * col_sin).astype(jnp.bfloat16)
+        xtab[0, row_im, :] = (-(cosine * col_sin) - sine * col_cos).astype(jnp.bfloat16)
+        return carry
 
     def x_table(p):
         x = lax.broadcasted_iota(jnp.int32, (deep, width), 1) * pieces + p
@@ -174,38 +200,50 @@
         lax.fori_loop(0, width // deep, strip_of, 0, unroll=True)
 
     with scope("xt0"):
-        x_table(0)
+        column = lax.broadcasted_iota(jnp.int32, (8, width), 1).astype(jnp.float32) * (turn_x * pieces)
+        column_sin, column_cos = turn_sincos(column)
+        vecs[0, :, :width] = column_cos
+        vecs[1, :, :width] = column_sin
+        col_cos = vecs[0, 0:1, :width]
+        col_sin = vecs[1, 0:1, :width]
+        lax.fori_loop(0, width // deep, x_first, 0, unroll=True)
 
     ytiles = short // LANES
 
     tall = short // YTALL
 
+    near_k = lax.broadcasted_iota(jnp.int32, (8, short), 1).astype(jnp.float32) * (1.0 / rows) + turn_y
+    turn_sin, turn_cos = turn_sincos(lax.broadcasted_iota(jnp.int32, (8, short), 0).astype(jnp.float32) * near_k)
+    vecs[0, :, :short] = turn_cos
+    vecs[1, :, :short] = turn_sin
+
     def y_table(step, carry):
-        n1 = step // (tall * ytiles)
-        strip = lax.rem(step // ytiles, tall)
+        strip = step // ytiles
         tile = lax.rem(step, ytiles)
-        n2 = lax.broadcasted_iota(jnp.int32, (YTALL, LANES), 0) + strip * YTALL
+        n2 = (lax.broadcasted_iota(jnp.int32, (YTALL, LANES), 0) + strip * YTALL).astype(jnp.float32)
         k2 = lax.broadcasted_iota(jnp.int32, (YTALL, LANES), 1) + tile * LANES
-        n = n2 * radix + n1
-        n = n.astype(jnp.float32)
-        turns = k2.astype(jnp.float32) * (n * (1.0 / rows))
+        turns = k2.astype(jnp.float32) * (n2 * (1.0 / short))
         turns = turns - jnp.floor(turns)
-        sine, cosine = turn_sincos(turns + n * turn_y + turn_0)
-        real = (wave_re * cosine + wave_im * sine).astype(jnp.bfloat16)
-        imag_f = wave_re * sine - wave_im * cosine
-        imag = imag_f.astype(jnp.bfloat16)
+        sine, cosine = turn_sincos(turns + n2 * (turn_y * radix) + turn_0)
+        real_0 = wave_re * cosine + wave_im * sine
+        imag_0 = wave_re * sine - wave_im * cosine
         top = pl.ds(pl.multiple_of(strip * YTALL, YTALL), YTALL)
         bottom = pl.ds(pl.multiple_of(strip * YTALL + short, YTALL), YTALL)
         left = pl.ds(pl.multiple_of(tile * LANES, LANES), LANES)
         right = pl.ds(pl.multiple_of(tile * LANES + short, LANES), LANES)
-        ytab[n1, top, left] = real
-        ytab[n1, top, right] = (-imag_f).astype(jnp.bfloat16)
-        ytab[n1, bottom, left] = imag
-        ytab[n1, bottom, right] = real
+        for n1 in range(radix):
+            turn_re = vecs[0, n1 : n1 + 1, left]
+            turn_im = vecs[1, n1 : n1 + 1, left]
+            real = (real_0 * turn_re - imag_0 * turn_im).astype(jnp.bfloat16)
+            imag = (real_0 * turn_im + imag_0 * turn_re).astype(jnp.bfloat16)
+            ytab[n1, top, left] = real
+            ytab[n1, top, right] = -imag
+            ytab[n1, bottom, left] = imag
+            ytab[n1, bottom, right] = real
         return carry
 
     with scope("ytab"):
-        lax.fori_loop(0, radix * tall * ytiles, y_table, 0, unroll=2)
+        lax.fori_loop(0, tall * ytiles, y_table, 0, unroll=2)
 
     half_gain = 0.5 * DEPTH_STEP * DEPTH_STEP
     step_y = 2.0 * math.pi / (rows * GRID_STEP) * math.sqrt(half_gain)
@@ -282,7 +320,7 @@
 
     with scope("factors"):
         factor_rows(rows // 16, put_middle)
-        lax.fori_loop(0, rows // 16, factors, middle, unroll=8)
+        lax.fori_loop(0, rows // 16, factors, middle, unroll=16)
 
     def shift(strip, total):
         rows_at = pl.ds(pl.multiple_of(strip * 16, 16), 16)
@@ -298,8 +336,11 @@
                 im = spec[1, k1, rows_at, at].astype(jnp.float32)
                 new_re = re * cosine - im * sine
                 new_im = re * sine + im * cosine
-                acc = acc + (new_re * new_re + new_im * new_im)
                 parts.append((new_re.astype(jnp.bfloat16), new_im.astype(jnp.bfloat16)))
+            powers = [re * re + im * im for re, im in parts]
+            while len(powers) > 1:
+                powers = [x + y for x, y in zip(powers[0::2], powers[1::2])]
+            acc = acc + powers[0].astype(jnp.float32)
             for n1, (re, im) in enumerate(butterfly(parts)):
                 zed[n1, rows_at, at] = re
                 low = pl.ds(pl.multiple_of(strip * 16 + short, 16), 16)
@@ -309,7 +350,7 @@
         return lax.fori_loop(0, tiles, inner, total, unroll=8)
 
     with scope("shift"):
-        pltpu.make_async_copy(spec_hbm, spec, load_sem).wait()
+        pltpu.make_async_copy(spec_hbm, spec.at[:, :, :, pl.ds(0, cols)], load_sem).wait()
         energy = lax.fori_loop(0, strips, shift, jnp.zeros((16, LANES), jnp.float32))
     etile[...] = energy[:8] + energy[8:]
 
@@ -351,7 +392,6 @@
         energy_copy(i).start()
         return carry
 
-    lax.fori_loop(1, groups, energy_start, 0)
 
     def ranked(j, count, centre):
         up = count - 1 - centre
@@ -564,6 +604,7 @@
 
         @pl.when(c == 0)
         def _():
+            lax.fori_loop(1, groups, energy_start, 0)
             with scope("xt"):
                 lax.fori_loop(1, pieces, lambda p, carry: (x_table(p), carry)[1], 0)
             take_core(c)
@@ -608,7 +649,7 @@
     part_lane = lanes8 // pieces
     lane_part = lax.rem(lanes8, pieces)
 
-    def own(p, carry):
+    def own(p, carry, last=False):
         cut = cut_of(p)
         with scope("oyw"):
             pair_copy(spot, p).wait_recv()
@@ -632,11 +673,17 @@
                 value = image[spot, pair, core, n1, :, source] * scale
                 spread = jnp.take_along_axis(value, part_lane + j % pieces * (LANES // pieces), axis=1)
                 to = slice(j * LANES, (j + 1) * LANES)
-                out_ref[:, n1, to] = jnp.where(lane_part == p, spread, out_ref[:, n1, to])
+                mine = jnp.where(lane_part == p, spread, mixed[n1, :, to])
+
+                if last:
+                    out_ref[:, n1, to] = mine
+                else:
+                    mixed[n1, :, to] = mine
         return carry
 
     with scope("own"):
-        lax.fori_loop(0, pieces, own, 0)
+        lax.fori_loop(0, pieces - 1, own, 0)
+        own(pieces - 1, 0, last=True)
 
     with scope("ownend"):
         all_sent(line_s, pair_in.at[1:lines])
@@ -657,18 +704,21 @@
         functools.partial(kernel, groups, radix, pieces, freq_total),
         out_shape=pltpu.VMEM((8, radix, cols), f32),
         in_specs=[
-            *[pl.BlockSpec(memory_space=pltpu.SMEM)] * 5,
-            pl.BlockSpec(memory_space=pl.ANY),
+            *[pl.BlockSpec(memory_space=pl.ANY)] * 6,
         ],
         out_specs=pl.BlockSpec(memory_space=pltpu.VMEM),
         scratch_shapes=[
-            pltpu.VMEM((2, radix, short, cols), bf16),
-            pltpu.VMEM((radix, 2 * short, cols), bf16),
+            *[pltpu.SMEM(small.shape, small.dtype) for small in (wavelet, freq_index, slowness, layer_ids, ray_slowness)],
+            pltpu.VMEM((2, radix, short, cols + LANES), bf16),
+            pltpu.VMEM((radix, 2 * short, cols + LANES), bf16),
             pltpu.VMEM((radix, 2 * short, 2 * short), bf16),
             pltpu.VMEM((pieces, groups // 2, radix, 16, 2 * (cols // pieces)), bf16),
             pltpu.VMEM((pieces, 2 * (cols // pieces), cols // pieces), bf16),
             pltpu.VMEM((pieces, 2 * short, cols // pieces), f32),
-            pltpu.VMEM((2, rows, cols), f32),
+            pltpu.VMEM((2, 8, max(short, cols // pieces)), f32),
+            pltpu.VMEM((2, cols // pieces, cols // pieces), f32),
+            pltpu.VMEM((2, rows + 8, cols + LANES), f32),
+            pltpu.VMEM((radix, 8, cols), f32),
             pltpu.VMEM((lines, 2, 2, radix, 8, cols), f32),
             pltpu.VMEM((lines, 2, radix, 8, cols), f32),
             pltpu.VMEM((lines, radix, 8, cols), f32),
@@ -677,6 +727,7 @@
             pltpu.VMEM((2, radix, 8, cols), f32),
             pltpu.VMEM((8, LANES), f32),
             pltpu.VMEM((groups, 8, LANES), f32),
+            dma((5,)),
             dma,
             dma,
             dma((min(lines, 4), pieces)),
@@ -692,7 +743,7 @@
             collective_id=0, has_side_effects=True, vmem_limit_bytes=60 * 1024 * 1024
         ),
     )(
-        wavelet, freq_index.reshape(1, 1), slowness, layer_ids.reshape(1, 1), ray_slowness,
+        wavelet, freq_index, slowness, layer_ids, ray_slowness,
         spectra.reshape(2, radix, short, cols),
     )
     return out.reshape(1, 8 * radix, cols)

time: 38.2 us -> 36 us (0.942)
  Pallas kernels: 35.9 us -> 33.8 us
    pallas_call x1, Pallas kernels: 35.9 us -> 33.8 us  [body(): pl.pallas_call(functools.partial(kernel, groups, radix, pieces, freq_tota...]
where the time goes in v4:
time: 36 us; the launch traced here: 35.8 us
  Pallas kernels  33.8 us (94%)
  between operations  1.3 us (4%)
  local copies, waits for them, and re-layouts  0.71 us (2%)
    pallas_call x1, Pallas kernels, body(): pl.pallas_call(functools.partial(kernel, groups, radix, pieces, freq_tota...  33.8 us

profile of v4, /device:TPU:0, one launch (start us, length us, event | category | flops | bytes accessed | tf_op | source)
XLA Modules:
  0.0 35.8 jit_solution(11915996764385295652)
XLA Ops:
  1.3 33.8 %shard_map.64 = f32[8,8,1024]{2,1,0:T(8,128)S(1)} custom-call(f32[1,2]{1,0:T(1,128)} %wavelet_hbm.1, s32[1]{0:T(128)S(6)} %copy.9.freq_hbm, f32[16]{0:T(128)} %slowness_hbm.1, s32[1]{0:T(128)S(6)} %copy.10.layer_hbm, f32[2]{0:T(128)} %rays_hbm.1, bf16[2,8,128,1024]{3,2,1,0:T(8,128)(2,1)} %bitcast.3), custom_call_target="tpu_custom_call" | custom-call | tf_op jit(solution)/shard_map/pallas_call | solution.py:703
  35.1 0.7 %copy.8 = f32[1,64,1024]{2,1,0:T(8,128)} copy(f32[1,64,1024]{2,1,0:T(8,128)S(1)} %bitcast.2) | data formatting | bytes 524288

commit v5 on v4

--- a/solution.py
+++ b/solution.py
@@ -94,7 +94,7 @@
     groups, radix, pieces, freq_total,
     wavelet_hbm, freq_hbm, slowness_hbm, layer_hbm, rays_hbm, spec_hbm, out_ref,
     wavelet, freq_index, slowness, layer_ids, rays,
-    spec, zed, ytab, field, xtab, yout, vecs, xbase, fac, mixed, image, core_in, pair_in, low_in, high_in, other_in, etile, eall,
+    spec, zed_a, zed_b, ytab, field, xtab, yout, vecs, xbase, fac, mixed, image, core_in, pair_in, low_in, high_in, other_in, etile, eall,
     small_sem, load_sem, core_s, core_r, pair_s, pair_r, line_s, line_r, other_r, e_s, e_r,
 ):
     rows = spec.shape[1] * spec.shape[2]
@@ -322,11 +322,18 @@
         factor_rows(rows // 16, put_middle)
         lax.fori_loop(0, rows // 16, factors, middle, unroll=16)
 
-    def shift(strip, total):
+    chips = groups // 2
+    half_width = width // 2
+    spread = half_width * pieces
+
+    def shift(strip, half_at, zed, acc):
         rows_at = pl.ds(pl.multiple_of(strip * 16, 16), 16)
-
-        def inner(tile, acc):
-            at = pl.ds(pl.multiple_of(tile * LANES, LANES), LANES)
+        low = pl.ds(pl.multiple_of(strip * 16 + short, 16), 16)
+        for tile in range(spread // LANES):
+            part, column = divmod(tile * LANES, half_width)
+            column = part * width + half_at * half_width + column
+            at = slice(column, column + LANES)
+            to = slice(tile * LANES, (tile + 1) * LANES)
             parts = []
             for k1 in range(radix):
                 row = pl.ds(pl.multiple_of(strip * 16 + k1 * short, 16), 16)
@@ -342,42 +349,49 @@
                 powers = [x + y for x, y in zip(powers[0::2], powers[1::2])]
             acc = acc + powers[0].astype(jnp.float32)
             for n1, (re, im) in enumerate(butterfly(parts)):
-                zed[n1, rows_at, at] = re
-                low = pl.ds(pl.multiple_of(strip * 16 + short, 16), 16)
-                zed[n1, low, at] = im
-            return acc
-
-        return lax.fori_loop(0, tiles, inner, total, unroll=8)
-
-    with scope("shift"):
-        pltpu.make_async_copy(spec_hbm, spec.at[:, :, :, pl.ds(0, cols)], load_sem).wait()
-        energy = lax.fori_loop(0, strips, shift, jnp.zeros((16, LANES), jnp.float32))
-    etile[...] = energy[:8] + energy[8:]
-
-    chips = groups // 2
-
-    def y_stage(n1, carry):
-        for part in range(pieces):
-            at = slice(part * width, (part + 1) * width)
-            yout[part] = jnp.dot(ytab[n1], zed[n1, :, at], preferred_element_type=jnp.float32)
+                zed[n1, rows_at, to] = re
+                zed[n1, low, to] = im
+        return acc
+
+    def y_stage(n1, half_at, zed):
+        slot = n1 % 2
+        for start in range(0, spread, 256):
+            at = slice(start, start + 256)
+            yout[slot, :, at] = jnp.dot(ytab[n1], zed[n1, :, at], preferred_element_type=jnp.float32)
 
         def fold(strip, inner):
             top = pl.ds(pl.multiple_of(strip * 16, 16), 16)
             low = pl.ds(pl.multiple_of(strip * 16 + short, 16), 16)
-            for lane_tile in range(width // LANES):
-                left = slice(lane_tile * LANES, (lane_tile + 1) * LANES)
-                right = slice(width + lane_tile * LANES, width + (lane_tile + 1) * LANES)
-                terms = [(yout[part, top, left], yout[part, low, left]) for part in range(pieces)]
+            for column in range(0, half_width, LANES):
+                left = slice(half_at * half_width + column, half_at * half_width + column + LANES)
+                right = slice(left.start + width, left.stop + width)
+                terms = []
+                for part in range(pieces):
+                    of = slice(part * half_width + column, part * half_width + column + LANES)
+                    terms.append((yout[slot, top, of], yout[slot, low, of]))
                 for x1, (re, im) in enumerate(butterfly(terms)):
                     field[x1, strip, n1, :, left] = re.astype(jnp.bfloat16)
                     field[x1, strip, n1, :, right] = im.astype(jnp.bfloat16)
             return inner
 
         lax.fori_loop(0, chips, fold, 0, unroll=True)
-        return carry
+
+    energy = jnp.zeros((16, LANES), jnp.float32)
+    with scope("shift"):
+        pltpu.make_async_copy(spec_hbm, spec.at[:, :, :, pl.ds(0, cols)], load_sem).wait()
+        energy = lax.fori_loop(0, strips, lambda i, acc: shift(i, 0, zed_a, acc), energy, unroll=2)
+    with scope("both"):
+        share = strips // radix
+        for n1 in range(radix):
+            energy = lax.fori_loop(
+                n1 * share, (n1 + 1) * share, lambda i, acc: shift(i, 1, zed_b, acc), energy, unroll=share == 1
+            )
+            y_stage(n1, 0, zed_a)
+    etile[...] = energy[:8] + energy[8:]
 
     with scope("ystage"):
-        lax.fori_loop(0, radix, y_stage, 0, unroll=True)
+        for n1 in range(radix):
+            y_stage(n1, 1, zed_b)
 
     with scope("barr"):
         pl.semaphore_wait(barrier, groups - 1)
@@ -710,11 +724,12 @@
         scratch_shapes=[
             *[pltpu.SMEM(small.shape, small.dtype) for small in (wavelet, freq_index, slowness, layer_ids, ray_slowness)],
             pltpu.VMEM((2, radix, short, cols + LANES), bf16),
-            pltpu.VMEM((radix, 2 * short, cols + LANES), bf16),
+            pltpu.VMEM((radix, 2 * short, cols // 2 + LANES), bf16),
+            pltpu.VMEM((radix, 2 * short, cols // 2 + LANES), bf16),
             pltpu.VMEM((radix, 2 * short, 2 * short), bf16),
             pltpu.VMEM((pieces, groups // 2, radix, 16, 2 * (cols // pieces)), bf16),
             pltpu.VMEM((pieces, 2 * (cols // pieces), cols // pieces), bf16),
-            pltpu.VMEM((pieces, 2 * short, cols // pieces), f32),
+            pltpu.VMEM((2, 2 * short, cols // 2), f32),
             pltpu.VMEM((2, 8, max(short, cols // pieces)), f32),
             pltpu.VMEM((2, cols // pieces, cols // pieces), f32),
             pltpu.VMEM((2, rows + 8, cols + LANES), f32),

time: 36 us -> 36.3 us (level)
  no operation moved by 1% of the time
where the time goes in v5:
time: 36.3 us; the launch traced here: 36.1 us
  Pallas kernels  34.1 us (94%)
  between operations  1.3 us (4%)
  local copies, waits for them, and re-layouts  0.71 us (2%)
    pallas_call x1, Pallas kernels, body(): pl.pallas_call(functools.partial(kernel, groups, radix, pieces, freq_tota...  34.1 us

profile of v5, /device:TPU:0, one launch (start us, length us, event | category | flops | bytes accessed | tf_op | source)
XLA Modules:
  0.0 36.1 jit_solution(16595834371456151099)
XLA Ops:
  1.3 34.1 %shard_map.64 = f32[8,8,1024]{2,1,0:T(8,128)S(1)} custom-call(f32[1,2]{1,0:T(1,128)} %wavelet_hbm.1, s32[1]{0:T(128)S(6)} %copy.9.freq_hbm, f32[16]{0:T(128)} %slowness_hbm.1, s32[1]{0:T(128)S(6)} %copy.10.layer_hbm, f32[2]{0:T(128)} %rays_hbm.1, bf16[2,8,128,1024]{3,2,1,0:T(8,128)(2,1)} %bitcast.3), custom_call_target="tpu_custom_call" | custom-call | tf_op jit(solution)/shard_map/pallas_call | solution.py:717
  35.4 0.7 %copy.8 = f32[1,64,1024]{2,1,0:T(8,128)} copy(f32[1,64,1024]{2,1,0:T(8,128)S(1)} %bitcast.2) | data formatting | bytes 524288
